TPU v7x, 32 devices: a whole 2x2x4 slice. The times are simulated.
32 devices in a mesh: shift: 4 (over y, core), band: 4 (over z), lane: 2 (over x).
Axes of the slice: x: 2, y: 2, z: 4, core: 2. Of those that a mesh axis runs over, the one named last changes fastest.
Arguments:
- source_terms: float32 [1024, 128, 128], P(('shift', 'band'), 'lane'), parts along dimension 0, may hold values from -6 to 6
- initial_values: float32 [1024, 128, 128], P(('shift', 'band'), 'lane'), parts along dimension 0, may hold values from -6 to 6
- absorption: float32 [1024, 128, 128], P(('shift', 'band'), 'lane'), parts along dimension 0, may hold values from 0.1 to 0.9
Outputs:
- corrected: float32 [1024, 128, 128], P(('shift', 'band'), 'lane'), parts along dimension 0
There are 4 independent parts, one for each index of `shift`. A program takes and returns all parts, laid end to end along the dimension named above; each array names one. Nothing has to cross between parts.
All inputs are finite; a program needn't handle non-finite values.
Results may differ from a plain program's by a relative error of at most 0.0003.
Values sent between devices are 32-bit elements.
A program may use at most 64 MiB of HBM per device.

v0:
```python
import jax
import jax.numpy as jnp
from jax import lax
from jax.sharding import PartitionSpec as P

RATIO = 2
BEFORE = 3
AFTER = 3
INNER = 13


def with_halo(block, sides, width, periodic):
    for axis, dim in sides:
        count = lax.axis_size(axis)
        forward = [(i, i + 1) for i in range(count - 1)]
        if periodic:
            forward.append((count - 1, 0))
        backward = [(target, source) for source, target in forward]
        low = lax.ppermute(
            lax.slice_in_dim(block, block.shape[dim] - width, None, axis=dim), axis, forward
        )
        high = lax.ppermute(lax.slice_in_dim(block, 0, width, axis=dim), axis, backward)
        block = jnp.concatenate([low, block, high], axis=dim)
    return block


def neighbour_sum(padded):
    inner_y, inner_x = (padded.shape[0] - 2, padded.shape[1] - 2)
    middle_rows = lax.slice_in_dim(padded, 1, 1 + inner_y, axis=0)
    middle_columns = lax.slice_in_dim(padded, 1, 1 + inner_x, axis=1)
    return (
        lax.slice_in_dim(middle_columns, 0, inner_y, axis=0)
        + lax.slice_in_dim(middle_columns, 2, 2 + inner_y, axis=0)
        + lax.slice_in_dim(middle_rows, 0, inner_x, axis=1)
        + lax.slice_in_dim(middle_rows, 2, 2 + inner_x, axis=1)
    )


def sweep_once(padded, values, load, mass_here):
    return values + 0.8 * (load + neighbour_sum(padded) - (4.0 + mass_here) * values) / (
        4.0 + mass_here
    )


def block_means(values):
    cut = values.reshape(
        values.shape[0] // RATIO, RATIO, values.shape[1] // RATIO, RATIO, values.shape[2]
    )
    return jnp.mean(cut, axis=(1, 3))


def spread_blocks(values):
    return jnp.repeat(jnp.repeat(values, RATIO, axis=0), RATIO, axis=1)


def without_rim(values):
    return lax.slice_in_dim(
        lax.slice_in_dim(values, 1, values.shape[0] - 1, axis=0), 1, values.shape[1] - 1, axis=1
    )


def per_device(source_terms, initial_values, absorption):
    values = initial_values
    for sweep in range(BEFORE):
        values = sweep_once(
            with_halo(values, (("band", 0), ("lane", 1)), 1, False),
            values,
            source_terms,
            absorption,
        )
    defect = (
        source_terms
        + neighbour_sum(with_halo(values, (("band", 0), ("lane", 1)), 1, False))
        - (4.0 + absorption) * values
    )
    coarse_load, coarse_mass = (block_means(defect) * RATIO, block_means(absorption) * RATIO)
    coarse_values = 0.8 * coarse_load / (4.0 + coarse_mass)
    depth = 2
    load_mass = with_halo(
        jnp.concatenate([coarse_load, coarse_mass], axis=2), (("band", 0), ("lane", 1)), 2, False
    )
    wide_load, wide_mass = jnp.split(load_mass, 2, axis=2)
    place_y = (
        lax.axis_index("band") * coarse_load.shape[0]
        - depth
        + jnp.arange(coarse_load.shape[0] + 2 * depth)
    )
    place_x = (
        lax.axis_index("lane") * coarse_load.shape[1]
        - depth
        + jnp.arange(coarse_load.shape[1] + 2 * depth)
    )
    inside_y = (place_y >= 0) & (place_y < coarse_load.shape[0] * lax.axis_size("band"))
    inside_x = (place_x >= 0) & (place_x < coarse_load.shape[1] * lax.axis_size("lane"))
    inside = (inside_y[:, None] & inside_x[None, :])[:, :, None]
    for group in range((INNER - 1) // 2):
        wide_values = with_halo(coarse_values, (("band", 0), ("lane", 1)), 2, False)
        once = sweep_once(
            wide_values, without_rim(wide_values), without_rim(wide_load), without_rim(wide_mass)
        )
        once = jnp.where(without_rim(inside), once, 0.0)
        middle = without_rim(once)
        coarse_values = sweep_once(once, middle, coarse_load, coarse_mass)
    values = values + spread_blocks(coarse_values)
    for sweep in range(AFTER):
        values = sweep_once(
            with_halo(values, (("band", 0), ("lane", 1)), 1, False),
            values,
            source_terms,
            absorption,
        )
    corrected = values
    return corrected


def solution(mesh):
    placed = (
        P(("shift", "band"), "lane", None),
        P(("shift", "band"), "lane", None),
        P(("shift", "band"), "lane", None),
    )
    return jax.shard_map(
        per_device,
        mesh=mesh,
        in_specs=placed,
        out_specs=P(("shift", "band"), "lane", None),
        check_vma=False,
    )
```

profile of v0, /device:TPU:0, one launch (start us, length us, event | category | flops | bytes accessed | tf_op | source)
XLA Modules:
  0.0 278.9 jit_solution(5512384404062238993)
XLA Ops:
  0.8 5.0 %collective-permute-start = (f32[1,64,128]{2,1,0:T(8,128)S(1)}, f32[1,64,128]{2,1,0:T(8,128)S(1)}, u32[]{:S(2)}, u32[]{:S(2)}) collective-permute-start(f32[1,64,128]{2,1,0:T(8,128)S(1)} %get-tuple-element.35), channel_id=1, source_target_pairs={{0,2},{2,4},{4,6},{1,3},{3,5},{5,7},{8,10},{10,12},{12,14},{9,11},... | collective-permute-start | bytes 98312 | tf_op jit(solution)/shard_map/ppermute | solution.py:19
  9.2 2.3 collective-permute-done.1
  11.6 3.4 %collective-permute-start.2 = (f32[66,1,128]{2,1,0:T(1,128)S(1)}, f32[66,1,128]{2,1,0:T(1,128)S(1)}, u32[]{:S(2)}, u32[]{:S(2)}) collective-permute-start(f32[66,1,128]{2,1,0:T(1,128)S(1)} %get-tuple-element.20), channel_id=1, source_target_pairs={{0,1},{2,3},{4,5},{6,7},{8,9},{10,11},{12,13},{14,15},{16,17},{18,... | collective-permute-start | bytes 101384 | tf_op jit(solution)/shard_map/ppermute | solution.py:19
  16.6 4.2 %collective-permute-done.3 = f32[66,1,128]{2,1,0:T(1,128)S(1)} collective-permute-done((f32[66,1,128]{2,1,0:T(1,128)S(1)}, f32[66,1,128]{2,1,0:T(1,128)S(1)}, u32[]{:S(2)}, u32[]{:S(2)}) %collective-permute-start.3) | collective-permute-done | bytes 33824 | tf_op jit(solution)/shard_map/ppermute | solution.py:22
  20.9 5.8 %fusion.50 = f32[64,64,128]{2,1,0:T(8,128)S(1)} fusion(f32[64,64,128]{2,1,0:T(8,128)} %param.4, f32[64,64,128]{2,1,0:T(8,128)S(1)} %copy-done.1, f32[66,1,128]{2,1,0:T(1,128)S(1)} %collective-permute-done.3, f32[66,64,128]{2,1,0:T(8,128)S(1)} %constant_dynamic-update-slice_fusion, f32[66,1,128]{2,1,0:T(1,128)S(1)} %collective-permute-done.2, ...), kind=kLoop, calls=%fused_computation.99 | loop fusion | flops 7340032 | bytes 10684416 | tf_op jit(solution)/shard_map/add | solution.py:40
  26.7 3.5 %collective-permute-start.4 = (f32[1,64,128]{2,1,0:T(8,128)S(1)}, f32[1,64,128]{2,1,0:T(8,128)S(1)}, u32[]{:S(2)}, u32[]{:S(2)}) collective-permute-start(f32[1,64,128]{2,1,0:T(8,128)S(1)} %get-tuple-element.32), channel_id=1, source_target_pairs={{0,2},{2,4},{4,6},{1,3},{3,5},{5,7},{8,10},{10,12},{12,14},{9,11},... | collective-permute-start | bytes 98312 | tf_op jit(solution)/shard_map/ppermute | solution.py:19
  31.8 4.2 %collective-permute-done.5 = f32[1,64,128]{2,1,0:T(8,128)S(1)} collective-permute-done((f32[1,64,128]{2,1,0:T(8,128)S(1)}, f32[1,64,128]{2,1,0:T(8,128)S(1)}, u32[]{:S(2)}, u32[]{:S(2)}) %collective-permute-start.5) | collective-permute-done | bytes 32800 | tf_op jit(solution)/shard_map/ppermute | solution.py:22
  39.2 4.2 %collective-permute-done.7 = f32[66,1,128]{2,1,0:T(1,128)S(1)} collective-permute-done((f32[66,1,128]{2,1,0:T(1,128)S(1)}, f32[66,1,128]{2,1,0:T(1,128)S(1)}, u32[]{:S(2)}, u32[]{:S(2)}) %collective-permute-start.7) | collective-permute-done | bytes 33824 | tf_op jit(solution)/shard_map/ppermute | solution.py:22
  43.5 8.6 %fusion.42 = f32[64,64,128]{2,1,0:T(8,128)S(1)} fusion(f32[64,64,128]{2,1,0:T(8,128)} %copy-done.7, f32[64,64,128]{2,1,0:T(8,128)} %param.3, f32[66,1,128]{2,1,0:T(1,128)S(1)} %collective-permute-done.7, f32[1,64,128]{2,1,0:T(8,128)S(1)} %collective-permute-done.5, f32[1,64,128]{2,1,0:T(8,128)S(1)} %collective-permute-done.4, ...), kind=kLoop, calls=%fused_computation.83 | loop fusion | flops 9437184 | bytes 8521728 | tf_op jit(solution)/shard_map/add | solution.py:40
  53.4 3.5 %collective-permute-start.8 = (f32[1,64,128]{2,1,0:T(8,128)S(1)}, f32[1,64,128]{2,1,0:T(8,128)S(1)}, u32[]{:S(2)}, u32[]{:S(2)}) collective-permute-start(f32[1,64,128]{2,1,0:T(8,128)S(1)} %get-tuple-element.30), channel_id=1, source_target_pairs={{0,2},{2,4},{4,6},{1,3},{3,5},{5,7},{8,10},{10,12},{12,14},{9,11},... | collective-permute-start | bytes 98312 | tf_op jit(solution)/shard_map/ppermute | solution.py:19
  58.5 4.2 %collective-permute-done.9 = f32[1,64,128]{2,1,0:T(8,128)S(1)} collective-permute-done((f32[1,64,128]{2,1,0:T(8,128)S(1)}, f32[1,64,128]{2,1,0:T(8,128)S(1)}, u32[]{:S(2)}, u32[]{:S(2)}) %collective-permute-start.9) | collective-permute-done | bytes 32800 | tf_op jit(solution)/shard_map/ppermute | solution.py:22
  67.0 4.2 %collective-permute-done.11 = f32[66,1,128]{2,1,0:T(1,128)S(1)} collective-permute-done((f32[66,1,128]{2,1,0:T(1,128)S(1)}, f32[66,1,128]{2,1,0:T(1,128)S(1)}, u32[]{:S(2)}, u32[]{:S(2)}) %collective-permute-start.11) | collective-permute-done | bytes 33824 | tf_op jit(solution)/shard_map/ppermute | solution.py:22
  71.3 8.0 %fusion.34 = f32[64,64,128]{2,1,0:T(8,128)S(1)} fusion(f32[64,64,128]{2,1,0:T(8,128)} %copy-done.6, f32[64,64,128]{2,1,0:T(8,128)S(1)} %copy-done.2, f32[66,1,128]{2,1,0:T(1,128)S(1)} %collective-permute-done.11, f32[1,64,128]{2,1,0:T(8,128)S(1)} %collective-permute-done.9, f32[1,64,128]{2,1,0:T(8,128)S(1)} %collective-permute-done.8, ...), kind=kLoop, calls=%fused_computation.67 | loop fusion | flops 9437184 | bytes 8521728 | tf_op jit(solution)/shard_map/add | solution.py:40
  79.3 2.0 collective-permute-start.12
  82.9 4.2 %collective-permute-done.13 = f32[1,64,128]{2,1,0:T(8,128)S(1)} collective-permute-done((f32[1,64,128]{2,1,0:T(8,128)S(1)}, f32[1,64,128]{2,1,0:T(8,128)S(1)}, u32[]{:S(2)}, u32[]{:S(2)}) %collective-permute-start.13) | collective-permute-done | bytes 32800 | tf_op jit(solution)/shard_map/ppermute | solution.py:22
  91.8 2.8 collective-permute-done.15
  94.6 9.3 %fusion.26 = f32[64,64,128]{2,1,0:T(8,128)} fusion(f32[64,64,128]{2,1,0:T(8,128)} %param.3, f32[66,1,128]{2,1,0:T(1,128)S(1)} %collective-permute-done.15, f32[1,64,128]{2,1,0:T(8,128)S(1)} %collective-permute-done.13, f32[64,64,128]{2,1,0:T(8,128)} %copy-done.4, f32[1,64,128]{2,1,0:T(8,128)S(1)} %collective-permute-done.12, ...), kind=kLoop, calls=%fused_computation.51 | loop fusion | flops 7864320 | bytes 8521728 | tf_op jit(solution)/shard_map/sub | solution.py:72
  103.9 3.2 %reduce_sum.18 = f32[32,32,128]{2,1,0:T(8,128)S(1)} reduce(f32[32,2,32,2,128]{4,3,2,1,0:T(2,128)} %bitcast.9, f32[]{:T(128)} %constant.35.clone.1), dimensions={1,3}, to_apply=%region_0.0 | reduce | flops 393216 | bytes 2621444 | tf_op jit(solution)/shard_map/reduce_sum | solution.py:49
  107.4 1.9 collective-permute-start.16
  110.7 4.5 %collective-permute-start.20 = (f32[2,32,256]{2,1,0:T(8,128)S(1)}, f32[2,32,256]{2,1,0:T(8,128)S(1)}, u32[]{:S(2)}, u32[]{:S(2)}) collective-permute-start(f32[2,32,256]{2,1,0:T(8,128)S(1)} %get-tuple-element.38), channel_id=1, source_target_pairs={{0,2},{2,4},{4,6},{1,3},{3,5},{5,7},{8,10},{10,12},{12,14},{9,11},... | collective-permute-start | bytes 196616 | tf_op jit(solution)/shard_map/ppermute | solution.py:19
  116.6 2.0 collective-permute-start.18
  121.4 3.1 %collective-permute-start.22 = (f32[36,2,256]{2,1,0:T(2,128)S(1)}, f32[36,2,256]{2,1,0:T(2,128)S(1)}, u32[]{:S(2)}, u32[]{:S(2)}) collective-permute-start(f32[36,2,256]{2,1,0:T(2,128)S(1)} %get-tuple-element.36), channel_id=1, source_target_pairs={{0,1},{2,3},{4,5},{6,7},{8,9},{10,11},{12,13},{14,15},{16,17},{18,... | collective-permute-start | bytes 221192 | tf_op jit(solution)/shard_map/ppermute | solution.py:19
  126.5 4.3 %collective-permute-done.23 = f32[36,2,256]{2,1,0:T(2,128)S(1)} collective-permute-done((f32[36,2,256]{2,1,0:T(2,128)S(1)}, f32[36,2,256]{2,1,0:T(2,128)S(1)}, u32[]{:S(2)}, u32[]{:S(2)}) %collective-permute-start.23) | collective-permute-done | bytes 73760 | tf_op jit(solution)/shard_map/ppermute | solution.py:22
  132.9 4.5 %collective-permute-start.24 = (f32[2,32,128]{2,1,0:T(8,128)S(1)}, f32[2,32,128]{2,1,0:T(8,128)S(1)}, u32[]{:S(2)}, u32[]{:S(2)}) collective-permute-start(f32[2,32,128]{2,1,0:T(8,128)S(1)} %get-tuple-element.60), channel_id=1, source_target_pairs={{0,2},{2,4},{4,6},{1,3},{3,5},{5,7},{8,10},{10,12},{12,14},{9,11},... | collective-permute-start | bytes 98312 | tf_op jit(solution)/shard_map/ppermute | solution.py:19
  139.1 4.2 %collective-permute-done.25 = f32[2,32,128]{2,1,0:T(8,128)S(1)} collective-permute-done((f32[2,32,128]{2,1,0:T(8,128)S(1)}, f32[2,32,128]{2,1,0:T(8,128)S(1)}, u32[]{:S(2)}, u32[]{:S(2)}) %collective-permute-start.25) | collective-permute-done | bytes 32800 | tf_op jit(solution)/shard_map/ppermute | solution.py:22
  146.5 4.3 %collective-permute-done.27 = f32[36,2,128]{2,1,0:T(2,128)S(1)} collective-permute-done((f32[36,2,128]{2,1,0:T(2,128)S(1)}, f32[36,2,128]{2,1,0:T(2,128)S(1)}, u32[]{:S(2)}, u32[]{:S(2)}) %collective-permute-start.27) | collective-permute-done | bytes 36896 | tf_op jit(solution)/shard_map/ppermute | solution.py:22
  155.8 4.2 %collective-permute-done.29 = f32[2,32,128]{2,1,0:T(8,128)S(1)} collective-permute-done((f32[2,32,128]{2,1,0:T(8,128)S(1)}, f32[2,32,128]{2,1,0:T(8,128)S(1)}, u32[]{:S(2)}, u32[]{:S(2)}) %collective-permute-start.29) | collective-permute-done | bytes 32800 | tf_op jit(solution)/shard_map/ppermute | solution.py:22
  163.4 4.2 %collective-permute-done.31 = f32[36,2,128]{2,1,0:T(2,128)S(1)} collective-permute-done((f32[36,2,128]{2,1,0:T(2,128)S(1)}, f32[36,2,128]{2,1,0:T(2,128)S(1)}, u32[]{:S(2)}, u32[]{:S(2)}) %collective-permute-start.31) | collective-permute-done | bytes 36896 | tf_op jit(solution)/shard_map/ppermute | solution.py:22
  169.2 2.2 collective-permute-start.32
  172.9 4.2 %collective-permute-done.33 = f32[2,32,128]{2,1,0:T(8,128)S(1)} collective-permute-done((f32[2,32,128]{2,1,0:T(8,128)S(1)}, f32[2,32,128]{2,1,0:T(8,128)S(1)}, u32[]{:S(2)}, u32[]{:S(2)}) %collective-permute-start.33) | collective-permute-done | bytes 32800 | tf_op jit(solution)/shard_map/ppermute | solution.py:22
  180.4 4.2 %collective-permute-done.35 = f32[36,2,128]{2,1,0:T(2,128)S(1)} collective-permute-done((f32[36,2,128]{2,1,0:T(2,128)S(1)}, f32[36,2,128]{2,1,0:T(2,128)S(1)}, u32[]{:S(2)}, u32[]{:S(2)}) %collective-permute-start.35) | collective-permute-done | bytes 36896 | tf_op jit(solution)/shard_map/ppermute | solution.py:22
  186.2 1.9 collective-permute-start.36
  189.7 4.2 %collective-permute-done.37 = f32[2,32,128]{2,1,0:T(8,128)S(1)} collective-permute-done((f32[2,32,128]{2,1,0:T(8,128)S(1)}, f32[2,32,128]{2,1,0:T(8,128)S(1)}, u32[]{:S(2)}, u32[]{:S(2)}) %collective-permute-start.37) | collective-permute-done | bytes 32800 | tf_op jit(solution)/shard_map/ppermute | solution.py:22
  197.2 4.2 %collective-permute-done.39 = f32[36,2,128]{2,1,0:T(2,128)S(1)} collective-permute-done((f32[36,2,128]{2,1,0:T(2,128)S(1)}, f32[36,2,128]{2,1,0:T(2,128)S(1)}, u32[]{:S(2)}, u32[]{:S(2)}) %collective-permute-start.39) | collective-permute-done | bytes 36896 | tf_op jit(solution)/shard_map/ppermute | solution.py:22
  202.9 1.9 collective-permute-start.40
  206.5 4.2 %collective-permute-done.41 = f32[2,32,128]{2,1,0:T(8,128)S(1)} collective-permute-done((f32[2,32,128]{2,1,0:T(8,128)S(1)}, f32[2,32,128]{2,1,0:T(8,128)S(1)}, u32[]{:S(2)}, u32[]{:S(2)}) %collective-permute-start.41) | collective-permute-done | bytes 32800 | tf_op jit(solution)/shard_map/ppermute | solution.py:22
  213.9 4.2 %collective-permute-done.43 = f32[36,2,128]{2,1,0:T(2,128)S(1)} collective-permute-done((f32[36,2,128]{2,1,0:T(2,128)S(1)}, f32[36,2,128]{2,1,0:T(2,128)S(1)}, u32[]{:S(2)}, u32[]{:S(2)}) %collective-permute-start.43) | collective-permute-done | bytes 36896 | tf_op jit(solution)/shard_map/ppermute | solution.py:22
  221.9 2.1 collective-permute-start.44
  225.5 4.2 %collective-permute-done.45 = f32[1,64,128]{2,1,0:T(8,128)S(1)} collective-permute-done((f32[1,64,128]{2,1,0:T(8,128)S(1)}, f32[1,64,128]{2,1,0:T(8,128)S(1)}, u32[]{:S(2)}, u32[]{:S(2)}) %collective-permute-start.45) | collective-permute-done | bytes 32800 | tf_op jit(solution)/shard_map/ppermute | solution.py:22
  233.0 4.2 %collective-permute-done.47 = f32[66,1,128]{2,1,0:T(1,128)S(1)} collective-permute-done((f32[66,1,128]{2,1,0:T(1,128)S(1)}, f32[66,1,128]{2,1,0:T(1,128)S(1)}, u32[]{:S(2)}, u32[]{:S(2)}) %collective-permute-start.47) | collective-permute-done | bytes 33824 | tf_op jit(solution)/shard_map/ppermute | solution.py:22
  237.2 3.4 %fusion.21 = f32[64,64,128]{2,1,0:T(8,128)S(1)} fusion(f32[64,64,128]{2,1,0:T(8,128)S(1)} %add.437, f32[64,64,128]{2,1,0:T(8,128)S(1)} %copy-done.3, f32[66,1,128]{2,1,0:T(1,128)S(1)} %collective-permute-done.47, f32[1,64,128]{2,1,0:T(8,128)S(1)} %collective-permute-done.45, f32[1,64,128]{2,1,0:T(8,128)S(1)} %collective-permute-done.44, ...), kind=kLoop, calls=%fused_computation.38 | loop fusion | flops 9437184 | bytes 8521728 | tf_op jit(solution)/shard_map/add | solution.py:40
  240.7 1.9 collective-permute-start.48
  244.2 4.2 %collective-permute-done.49 = f32[1,64,128]{2,1,0:T(8,128)S(1)} collective-permute-done((f32[1,64,128]{2,1,0:T(8,128)S(1)}, f32[1,64,128]{2,1,0:T(8,128)S(1)}, u32[]{:S(2)}, u32[]{:S(2)}) %collective-permute-start.49) | collective-permute-done | bytes 32800 | tf_op jit(solution)/shard_map/ppermute | solution.py:22
  251.7 4.2 %collective-permute-done.51 = f32[66,1,128]{2,1,0:T(1,128)S(1)} collective-permute-done((f32[66,1,128]{2,1,0:T(1,128)S(1)}, f32[66,1,128]{2,1,0:T(1,128)S(1)}, u32[]{:S(2)}, u32[]{:S(2)}) %collective-permute-start.51) | collective-permute-done | bytes 33824 | tf_op jit(solution)/shard_map/ppermute | solution.py:22
  255.9 3.4 %fusion.13 = f32[64,64,128]{2,1,0:T(8,128)S(1)} fusion(f32[64,64,128]{2,1,0:T(8,128)S(1)} %fusion.21, f32[64,64,128]{2,1,0:T(8,128)S(1)} %copy-done.3, f32[66,1,128]{2,1,0:T(1,128)S(1)} %collective-permute-done.51, f32[1,64,128]{2,1,0:T(8,128)S(1)} %collective-permute-done.49, f32[1,64,128]{2,1,0:T(8,128)S(1)} %collective-permute-done.48, ...), kind=kLoop, calls=%fused_computation.22 | loop fusion | flops 9437184 | bytes 8521728 | tf_op jit(solution)/shard_map/add | solution.py:40
  262.8 4.2 %collective-permute-done.53 = f32[1,64,128]{2,1,0:T(8,128)S(1)} collective-permute-done((f32[1,64,128]{2,1,0:T(8,128)S(1)}, f32[1,64,128]{2,1,0:T(8,128)S(1)}, u32[]{:S(2)}, u32[]{:S(2)}) %collective-permute-start.53) | collective-permute-done | bytes 32800 | tf_op jit(solution)/shard_map/ppermute | solution.py:22
  270.3 4.2 %collective-permute-done.55 = f32[66,1,128]{2,1,0:T(1,128)S(1)} collective-permute-done((f32[66,1,128]{2,1,0:T(1,128)S(1)}, f32[66,1,128]{2,1,0:T(1,128)S(1)}, u32[]{:S(2)}, u32[]{:S(2)}) %collective-permute-start.55) | collective-permute-done | bytes 33824 | tf_op jit(solution)/shard_map/ppermute | solution.py:22
  274.5 4.3 %fusion.5 = f32[64,64,128]{2,1,0:T(8,128)} fusion(f32[64,64,128]{2,1,0:T(8,128)S(1)} %fusion.13, f32[64,64,128]{2,1,0:T(8,128)S(1)} %copy-done.3, f32[66,1,128]{2,1,0:T(1,128)S(1)} %collective-permute-done.55, f32[1,64,128]{2,1,0:T(8,128)S(1)} %collective-permute-done.53, f32[1,64,128]{2,1,0:T(8,128)S(1)} %collective-permute-done.52, ...), kind=kLoop, calls=%fused_computation.6 | loop fusion | flops 9437184 | bytes 8521728 | tf_op jit(solution)/shard_map/add | solution.py:40
  (147 shorter events, 85.9 us)
Async XLA Ops:
  0.8 6.6 %collective-permute-start = (f32[1,64,128]{2,1,0:T(8,128)S(1)}, f32[1,64,128]{2,1,0:T(8,128)S(1)}, u32[]{:S(2)}, u32[]{:S(2)}) collective-permute-start(f32[1,64,128]{2,1,0:T(8,128)S(1)} %get-tuple-element.35), channel_id=1, source_target_pairs={{0,2},{2,4},{4,6},{1,3},{3,5},{5,7},{8,10},{10,12},{12,14},{9,11},... | collective-permute-start | bytes 98312 | tf_op jit(solution)/shard_map/ppermute | solution.py:19
  5.8 5.8 %collective-permute-start.1 = (f32[1,64,128]{2,1,0:T(8,128)S(1)}, f32[1,64,128]{2,1,0:T(8,128)S(1)}, u32[]{:S(2)}, u32[]{:S(2)}) collective-permute-start(f32[1,64,128]{2,1,0:T(8,128)S(1)} %get-tuple-element.34), channel_id=1, source_target_pairs={{2,0},{4,2},{6,4},{3,1},{5,3},{7,5},{10,8},{12,10},{14,12},{11,9},... | collective-permute-start | bytes 98312 | tf_op jit(solution)/shard_map/ppermute | solution.py:22
  11.6 5.0 %collective-permute-start.2 = (f32[66,1,128]{2,1,0:T(1,128)S(1)}, f32[66,1,128]{2,1,0:T(1,128)S(1)}, u32[]{:S(2)}, u32[]{:S(2)}) collective-permute-start(f32[66,1,128]{2,1,0:T(1,128)S(1)} %get-tuple-element.20), channel_id=1, source_target_pairs={{0,1},{2,3},{4,5},{6,7},{8,9},{10,11},{12,13},{14,15},{16,17},{18,... | collective-permute-start | bytes 101384 | tf_op jit(solution)/shard_map/ppermute | solution.py:19
  15.0 5.8 %collective-permute-start.3 = (f32[66,1,128]{2,1,0:T(1,128)S(1)}, f32[66,1,128]{2,1,0:T(1,128)S(1)}, u32[]{:S(2)}, u32[]{:S(2)}) collective-permute-start(f32[66,1,128]{2,1,0:T(1,128)S(1)} %get-tuple-element.21), channel_id=1, source_target_pairs={{1,0},{3,2},{5,4},{7,6},{9,8},{11,10},{13,12},{15,14},{17,16},{19,... | collective-permute-start | bytes 101384 | tf_op jit(solution)/shard_map/ppermute | solution.py:22
  26.7 5.1 %collective-permute-start.4 = (f32[1,64,128]{2,1,0:T(8,128)S(1)}, f32[1,64,128]{2,1,0:T(8,128)S(1)}, u32[]{:S(2)}, u32[]{:S(2)}) collective-permute-start(f32[1,64,128]{2,1,0:T(8,128)S(1)} %get-tuple-element.32), channel_id=1, source_target_pairs={{0,2},{2,4},{4,6},{1,3},{3,5},{5,7},{8,10},{10,12},{12,14},{9,11},... | collective-permute-start | bytes 98312 | tf_op jit(solution)/shard_map/ppermute | solution.py:19
  30.2 5.8 %collective-permute-start.5 = (f32[1,64,128]{2,1,0:T(8,128)S(1)}, f32[1,64,128]{2,1,0:T(8,128)S(1)}, u32[]{:S(2)}, u32[]{:S(2)}) collective-permute-start(f32[1,64,128]{2,1,0:T(8,128)S(1)} %get-tuple-element.33), channel_id=1, source_target_pairs={{2,0},{4,2},{6,4},{3,1},{5,3},{7,5},{10,8},{12,10},{14,12},{11,9},... | collective-permute-start | bytes 98312 | tf_op jit(solution)/shard_map/ppermute | solution.py:22
  37.7 5.8 %collective-permute-start.7 = (f32[66,1,128]{2,1,0:T(1,128)S(1)}, f32[66,1,128]{2,1,0:T(1,128)S(1)}, u32[]{:S(2)}, u32[]{:S(2)}) collective-permute-start(f32[66,1,128]{2,1,0:T(1,128)S(1)} %get-tuple-element.19), channel_id=1, source_target_pairs={{1,0},{3,2},{5,4},{7,6},{9,8},{11,10},{13,12},{15,14},{17,16},{19,... | collective-permute-start | bytes 101384 | tf_op jit(solution)/shard_map/ppermute | solution.py:22
  53.4 5.1 %collective-permute-start.8 = (f32[1,64,128]{2,1,0:T(8,128)S(1)}, f32[1,64,128]{2,1,0:T(8,128)S(1)}, u32[]{:S(2)}, u32[]{:S(2)}) collective-permute-start(f32[1,64,128]{2,1,0:T(8,128)S(1)} %get-tuple-element.30), channel_id=1, source_target_pairs={{0,2},{2,4},{4,6},{1,3},{3,5},{5,7},{8,10},{10,12},{12,14},{9,11},... | collective-permute-start | bytes 98312 | tf_op jit(solution)/shard_map/ppermute | solution.py:19
  56.9 5.8 %collective-permute-start.9 = (f32[1,64,128]{2,1,0:T(8,128)S(1)}, f32[1,64,128]{2,1,0:T(8,128)S(1)}, u32[]{:S(2)}, u32[]{:S(2)}) collective-permute-start(f32[1,64,128]{2,1,0:T(8,128)S(1)} %get-tuple-element.31), channel_id=1, source_target_pairs={{2,0},{4,2},{6,4},{3,1},{5,3},{7,5},{10,8},{12,10},{14,12},{11,9},... | collective-permute-start | bytes 98312 | tf_op jit(solution)/shard_map/ppermute | solution.py:22
  65.4 5.8 %collective-permute-start.11 = (f32[66,1,128]{2,1,0:T(1,128)S(1)}, f32[66,1,128]{2,1,0:T(1,128)S(1)}, u32[]{:S(2)}, u32[]{:S(2)}) collective-permute-start(f32[66,1,128]{2,1,0:T(1,128)S(1)} %get-tuple-element.17), channel_id=1, source_target_pairs={{1,0},{3,2},{5,4},{7,6},{9,8},{11,10},{13,12},{15,14},{17,16},{19,... | collective-permute-start | bytes 101384 | tf_op jit(solution)/shard_map/ppermute | solution.py:22
  79.3 3.6 %collective-permute-start.12 = (f32[1,64,128]{2,1,0:T(8,128)S(1)}, f32[1,64,128]{2,1,0:T(8,128)S(1)}, u32[]{:S(2)}, u32[]{:S(2)}) collective-permute-start(f32[1,64,128]{2,1,0:T(8,128)S(1)} %get-tuple-element.28), channel_id=1, source_target_pairs={{0,2},{2,4},{4,6},{1,3},{3,5},{5,7},{8,10},{10,12},{12,14},{9,11},... | collective-permute-start | bytes 98312 | tf_op jit(solution)/shard_map/ppermute | solution.py:19
  81.3 5.8 %collective-permute-start.13 = (f32[1,64,128]{2,1,0:T(8,128)S(1)}, f32[1,64,128]{2,1,0:T(8,128)S(1)}, u32[]{:S(2)}, u32[]{:S(2)}) collective-permute-start(f32[1,64,128]{2,1,0:T(8,128)S(1)} %get-tuple-element.29), channel_id=1, source_target_pairs={{2,0},{4,2},{6,4},{3,1},{5,3},{7,5},{10,8},{12,10},{14,12},{11,9},... | collective-permute-start | bytes 98312 | tf_op jit(solution)/shard_map/ppermute | solution.py:22
  87.2 4.6 %collective-permute-start.14 = (f32[66,1,128]{2,1,0:T(1,128)S(1)}, f32[66,1,128]{2,1,0:T(1,128)S(1)}, u32[]{:S(2)}, u32[]{:S(2)}) collective-permute-start(f32[66,1,128]{2,1,0:T(1,128)S(1)} %get-tuple-element.14), channel_id=1, source_target_pairs={{0,1},{2,3},{4,5},{6,7},{8,9},{10,11},{12,13},{14,15},{16,17},{18,... | collective-permute-start | bytes 101384 | tf_op jit(solution)/shard_map/ppermute | solution.py:19
  88.8 5.8 %collective-permute-start.15 = (f32[66,1,128]{2,1,0:T(1,128)S(1)}, f32[66,1,128]{2,1,0:T(1,128)S(1)}, u32[]{:S(2)}, u32[]{:S(2)}) collective-permute-start(f32[66,1,128]{2,1,0:T(1,128)S(1)} %get-tuple-element.15), channel_id=1, source_target_pairs={{1,0},{3,2},{5,4},{7,6},{9,8},{11,10},{13,12},{15,14},{17,16},{19,... | collective-permute-start | bytes 101384 | tf_op jit(solution)/shard_map/ppermute | solution.py:22
  107.4 9.1 %collective-permute-start.16 = (f32[2,32,128]{2,1,0:T(8,128)S(1)}, f32[2,32,128]{2,1,0:T(8,128)S(1)}, u32[]{:S(2)}, u32[]{:S(2)}) collective-permute-start(f32[2,32,128]{2,1,0:T(8,128)S(1)} %get-tuple-element.65), channel_id=1, source_target_pairs={{0,2},{2,4},{4,6},{1,3},{3,5},{5,7},{8,10},{10,12},{12,14},{9,11},... | collective-permute-start | bytes 98312 | tf_op jit(solution)/shard_map/ppermute | solution.py:19
  109.3 7.2 %collective-permute-start.17 = (f32[2,32,128]{2,1,0:T(8,128)S(1)}, f32[2,32,128]{2,1,0:T(8,128)S(1)}, u32[]{:S(2)}, u32[]{:S(2)}) collective-permute-start(f32[2,32,128]{2,1,0:T(8,128)S(1)} %get-tuple-element.66), channel_id=1, source_target_pairs={{2,0},{4,2},{6,4},{3,1},{5,3},{7,5},{10,8},{12,10},{14,12},{11,9},... | collective-permute-start | bytes 98312 | tf_op jit(solution)/shard_map/ppermute | solution.py:22
  110.7 9.2 %collective-permute-start.20 = (f32[2,32,256]{2,1,0:T(8,128)S(1)}, f32[2,32,256]{2,1,0:T(8,128)S(1)}, u32[]{:S(2)}, u32[]{:S(2)}) collective-permute-start(f32[2,32,256]{2,1,0:T(8,128)S(1)} %get-tuple-element.38), channel_id=1, source_target_pairs={{0,2},{2,4},{4,6},{1,3},{3,5},{5,7},{8,10},{10,12},{12,14},{9,11},... | collective-permute-start | bytes 196616 | tf_op jit(solution)/shard_map/ppermute | solution.py:19
  115.2 6.2 %collective-permute-start.21 = (f32[2,32,256]{2,1,0:T(8,128)S(1)}, f32[2,32,256]{2,1,0:T(8,128)S(1)}, u32[]{:S(2)}, u32[]{:S(2)}) collective-permute-start(f32[2,32,256]{2,1,0:T(8,128)S(1)} %get-tuple-element.39), channel_id=1, source_target_pairs={{2,0},{4,2},{6,4},{3,1},{5,3},{7,5},{10,8},{12,10},{14,12},{11,9},... | collective-permute-start | bytes 196616 | tf_op jit(solution)/shard_map/ppermute | solution.py:22
  116.6 9.2 %collective-permute-start.18 = (f32[36,2,128]{2,1,0:T(2,128)S(1)}, f32[36,2,128]{2,1,0:T(2,128)S(1)}, u32[]{:S(2)}, u32[]{:S(2)}) collective-permute-start(f32[36,2,128]{2,1,0:T(2,128)S(1)} %get-tuple-element.50), channel_id=1, source_target_pairs={{0,1},{2,3},{4,5},{6,7},{8,9},{10,11},{12,13},{14,15},{16,17},{18,... | collective-permute-start | bytes 110600 | tf_op jit(solution)/shard_map/ppermute | solution.py:19
  118.6 7.3 %collective-permute-start.19 = (f32[36,2,128]{2,1,0:T(2,128)S(1)}, f32[36,2,128]{2,1,0:T(2,128)S(1)}, u32[]{:S(2)}, u32[]{:S(2)}) collective-permute-start(f32[36,2,128]{2,1,0:T(2,128)S(1)} %get-tuple-element.51), channel_id=1, source_target_pairs={{1,0},{3,2},{5,4},{7,6},{9,8},{11,10},{13,12},{15,14},{17,16},{19,... | collective-permute-start | bytes 110600 | tf_op jit(solution)/shard_map/ppermute | solution.py:22
  121.4 5.0 %collective-permute-start.22 = (f32[36,2,256]{2,1,0:T(2,128)S(1)}, f32[36,2,256]{2,1,0:T(2,128)S(1)}, u32[]{:S(2)}, u32[]{:S(2)}) collective-permute-start(f32[36,2,256]{2,1,0:T(2,128)S(1)} %get-tuple-element.36), channel_id=1, source_target_pairs={{0,1},{2,3},{4,5},{6,7},{8,9},{10,11},{12,13},{14,15},{16,17},{18,... | collective-permute-start | bytes 221192 | tf_op jit(solution)/shard_map/ppermute | solution.py:19
  124.5 6.2 %collective-permute-start.23 = (f32[36,2,256]{2,1,0:T(2,128)S(1)}, f32[36,2,256]{2,1,0:T(2,128)S(1)}, u32[]{:S(2)}, u32[]{:S(2)}) collective-permute-start(f32[36,2,256]{2,1,0:T(2,128)S(1)} %get-tuple-element.37), channel_id=1, source_target_pairs={{1,0},{3,2},{5,4},{7,6},{9,8},{11,10},{13,12},{15,14},{17,16},{19,... | collective-permute-start | bytes 221192 | tf_op jit(solution)/shard_map/ppermute | solution.py:22
  132.9 6.1 %collective-permute-start.24 = (f32[2,32,128]{2,1,0:T(8,128)S(1)}, f32[2,32,128]{2,1,0:T(8,128)S(1)}, u32[]{:S(2)}, u32[]{:S(2)}) collective-permute-start(f32[2,32,128]{2,1,0:T(8,128)S(1)} %get-tuple-element.60), channel_id=1, source_target_pairs={{0,2},{2,4},{4,6},{1,3},{3,5},{5,7},{8,10},{10,12},{12,14},{9,11},... | collective-permute-start | bytes 98312 | tf_op jit(solution)/shard_map/ppermute | solution.py:19
  137.5 5.8 %collective-permute-start.25 = (f32[2,32,128]{2,1,0:T(8,128)S(1)}, f32[2,32,128]{2,1,0:T(8,128)S(1)}, u32[]{:S(2)}, u32[]{:S(2)}) collective-permute-start(f32[2,32,128]{2,1,0:T(8,128)S(1)} %get-tuple-element.61), channel_id=1, source_target_pairs={{2,0},{4,2},{6,4},{3,1},{5,3},{7,5},{10,8},{12,10},{14,12},{11,9},... | collective-permute-start | bytes 98312 | tf_op jit(solution)/shard_map/ppermute | solution.py:22
  144.9 5.9 %collective-permute-start.27 = (f32[36,2,128]{2,1,0:T(2,128)S(1)}, f32[36,2,128]{2,1,0:T(2,128)S(1)}, u32[]{:S(2)}, u32[]{:S(2)}) collective-permute-start(f32[36,2,128]{2,1,0:T(2,128)S(1)} %get-tuple-element.49), channel_id=1, source_target_pairs={{1,0},{3,2},{5,4},{7,6},{9,8},{11,10},{13,12},{15,14},{17,16},{19,... | collective-permute-start | bytes 110600 | tf_op jit(solution)/shard_map/ppermute | solution.py:22
  152.4 3.4 %collective-permute-start.28 = (f32[2,32,128]{2,1,0:T(8,128)S(1)}, f32[2,32,128]{2,1,0:T(8,128)S(1)}, u32[]{:S(2)}, u32[]{:S(2)}) collective-permute-start(f32[2,32,128]{2,1,0:T(8,128)S(1)} %get-tuple-element.58), channel_id=1, source_target_pairs={{0,2},{2,4},{4,6},{1,3},{3,5},{5,7},{8,10},{10,12},{12,14},{9,11},... | collective-permute-start | bytes 98312 | tf_op jit(solution)/shard_map/ppermute | solution.py:19
  154.2 5.8 %collective-permute-start.29 = (f32[2,32,128]{2,1,0:T(8,128)S(1)}, f32[2,32,128]{2,1,0:T(8,128)S(1)}, u32[]{:S(2)}, u32[]{:S(2)}) collective-permute-start(f32[2,32,128]{2,1,0:T(8,128)S(1)} %get-tuple-element.59), channel_id=1, source_target_pairs={{2,0},{4,2},{6,4},{3,1},{5,3},{7,5},{10,8},{12,10},{14,12},{11,9},... | collective-permute-start | bytes 98312 | tf_op jit(solution)/shard_map/ppermute | solution.py:22
  160.1 3.3 %collective-permute-start.30 = (f32[36,2,128]{2,1,0:T(2,128)S(1)}, f32[36,2,128]{2,1,0:T(2,128)S(1)}, u32[]{:S(2)}, u32[]{:S(2)}) collective-permute-start(f32[36,2,128]{2,1,0:T(2,128)S(1)} %get-tuple-element.46), channel_id=1, source_target_pairs={{0,1},{2,3},{4,5},{6,7},{8,9},{10,11},{12,13},{14,15},{16,17},{18,... | collective-permute-start | bytes 110600 | tf_op jit(solution)/shard_map/ppermute | solution.py:19
  161.8 5.9 %collective-permute-start.31 = (f32[36,2,128]{2,1,0:T(2,128)S(1)}, f32[36,2,128]{2,1,0:T(2,128)S(1)}, u32[]{:S(2)}, u32[]{:S(2)}) collective-permute-start(f32[36,2,128]{2,1,0:T(2,128)S(1)} %get-tuple-element.47), channel_id=1, source_target_pairs={{1,0},{3,2},{5,4},{7,6},{9,8},{11,10},{13,12},{15,14},{17,16},{19,... | collective-permute-start | bytes 110600 | tf_op jit(solution)/shard_map/ppermute | solution.py:22
  169.2 3.7 %collective-permute-start.32 = (f32[2,32,128]{2,1,0:T(8,128)S(1)}, f32[2,32,128]{2,1,0:T(8,128)S(1)}, u32[]{:S(2)}, u32[]{:S(2)}) collective-permute-start(f32[2,32,128]{2,1,0:T(8,128)S(1)} %get-tuple-element.56), channel_id=1, source_target_pairs={{0,2},{2,4},{4,6},{1,3},{3,5},{5,7},{8,10},{10,12},{12,14},{9,11},... | collective-permute-start | bytes 98312 | tf_op jit(solution)/shard_map/ppermute | solution.py:19
  171.3 5.8 %collective-permute-start.33 = (f32[2,32,128]{2,1,0:T(8,128)S(1)}, f32[2,32,128]{2,1,0:T(8,128)S(1)}, u32[]{:S(2)}, u32[]{:S(2)}) collective-permute-start(f32[2,32,128]{2,1,0:T(8,128)S(1)} %get-tuple-element.57), channel_id=1, source_target_pairs={{2,0},{4,2},{6,4},{3,1},{5,3},{7,5},{10,8},{12,10},{14,12},{11,9},... | collective-permute-start | bytes 98312 | tf_op jit(solution)/shard_map/ppermute | solution.py:22
  178.8 5.9 %collective-permute-start.35 = (f32[36,2,128]{2,1,0:T(2,128)S(1)}, f32[36,2,128]{2,1,0:T(2,128)S(1)}, u32[]{:S(2)}, u32[]{:S(2)}) collective-permute-start(f32[36,2,128]{2,1,0:T(2,128)S(1)} %get-tuple-element.45), channel_id=1, source_target_pairs={{1,0},{3,2},{5,4},{7,6},{9,8},{11,10},{13,12},{15,14},{17,16},{19,... | collective-permute-start | bytes 110600 | tf_op jit(solution)/shard_map/ppermute | solution.py:22
  186.2 3.5 %collective-permute-start.36 = (f32[2,32,128]{2,1,0:T(8,128)S(1)}, f32[2,32,128]{2,1,0:T(8,128)S(1)}, u32[]{:S(2)}, u32[]{:S(2)}) collective-permute-start(f32[2,32,128]{2,1,0:T(8,128)S(1)} %get-tuple-element.54), channel_id=1, source_target_pairs={{0,2},{2,4},{4,6},{1,3},{3,5},{5,7},{8,10},{10,12},{12,14},{9,11},... | collective-permute-start | bytes 98312 | tf_op jit(solution)/shard_map/ppermute | solution.py:19
  188.1 5.8 %collective-permute-start.37 = (f32[2,32,128]{2,1,0:T(8,128)S(1)}, f32[2,32,128]{2,1,0:T(8,128)S(1)}, u32[]{:S(2)}, u32[]{:S(2)}) collective-permute-start(f32[2,32,128]{2,1,0:T(8,128)S(1)} %get-tuple-element.55), channel_id=1, source_target_pairs={{2,0},{4,2},{6,4},{3,1},{5,3},{7,5},{10,8},{12,10},{14,12},{11,9},... | collective-permute-start | bytes 98312 | tf_op jit(solution)/shard_map/ppermute | solution.py:22
  193.9 3.2 %collective-permute-start.38 = (f32[36,2,128]{2,1,0:T(2,128)S(1)}, f32[36,2,128]{2,1,0:T(2,128)S(1)}, u32[]{:S(2)}, u32[]{:S(2)}) collective-permute-start(f32[36,2,128]{2,1,0:T(2,128)S(1)} %get-tuple-element.42), channel_id=1, source_target_pairs={{0,1},{2,3},{4,5},{6,7},{8,9},{10,11},{12,13},{14,15},{16,17},{18,... | collective-permute-start | bytes 110600 | tf_op jit(solution)/shard_map/ppermute | solution.py:19
  195.6 5.9 %collective-permute-start.39 = (f32[36,2,128]{2,1,0:T(2,128)S(1)}, f32[36,2,128]{2,1,0:T(2,128)S(1)}, u32[]{:S(2)}, u32[]{:S(2)}) collective-permute-start(f32[36,2,128]{2,1,0:T(2,128)S(1)} %get-tuple-element.43), channel_id=1, source_target_pairs={{1,0},{3,2},{5,4},{7,6},{9,8},{11,10},{13,12},{15,14},{17,16},{19,... | collective-permute-start | bytes 110600 | tf_op jit(solution)/shard_map/ppermute | solution.py:22
  202.9 3.5 %collective-permute-start.40 = (f32[2,32,128]{2,1,0:T(8,128)S(1)}, f32[2,32,128]{2,1,0:T(8,128)S(1)}, u32[]{:S(2)}, u32[]{:S(2)}) collective-permute-start(f32[2,32,128]{2,1,0:T(8,128)S(1)} %get-tuple-element.52), channel_id=1, source_target_pairs={{0,2},{2,4},{4,6},{1,3},{3,5},{5,7},{8,10},{10,12},{12,14},{9,11},... | collective-permute-start | bytes 98312 | tf_op jit(solution)/shard_map/ppermute | solution.py:19
  204.9 5.8 %collective-permute-start.41 = (f32[2,32,128]{2,1,0:T(8,128)S(1)}, f32[2,32,128]{2,1,0:T(8,128)S(1)}, u32[]{:S(2)}, u32[]{:S(2)}) collective-permute-start(f32[2,32,128]{2,1,0:T(8,128)S(1)} %get-tuple-element.53), channel_id=1, source_target_pairs={{2,0},{4,2},{6,4},{3,1},{5,3},{7,5},{10,8},{12,10},{14,12},{11,9},... | collective-permute-start | bytes 98312 | tf_op jit(solution)/shard_map/ppermute | solution.py:22
  212.3 5.9 %collective-permute-start.43 = (f32[36,2,128]{2,1,0:T(2,128)S(1)}, f32[36,2,128]{2,1,0:T(2,128)S(1)}, u32[]{:S(2)}, u32[]{:S(2)}) collective-permute-start(f32[36,2,128]{2,1,0:T(2,128)S(1)} %get-tuple-element.41), channel_id=1, source_target_pairs={{1,0},{3,2},{5,4},{7,6},{9,8},{11,10},{13,12},{15,14},{17,16},{19,... | collective-permute-start | bytes 110600 | tf_op jit(solution)/shard_map/ppermute | solution.py:22
  221.9 3.6 %collective-permute-start.44 = (f32[1,64,128]{2,1,0:T(8,128)S(1)}, f32[1,64,128]{2,1,0:T(8,128)S(1)}, u32[]{:S(2)}, u32[]{:S(2)}) collective-permute-start(f32[1,64,128]{2,1,0:T(8,128)S(1)} %get-tuple-element.26), channel_id=1, source_target_pairs={{0,2},{2,4},{4,6},{1,3},{3,5},{5,7},{8,10},{10,12},{12,14},{9,11},... | collective-permute-start | bytes 98312 | tf_op jit(solution)/shard_map/ppermute | solution.py:19
  223.9 5.8 %collective-permute-start.45 = (f32[1,64,128]{2,1,0:T(8,128)S(1)}, f32[1,64,128]{2,1,0:T(8,128)S(1)}, u32[]{:S(2)}, u32[]{:S(2)}) collective-permute-start(f32[1,64,128]{2,1,0:T(8,128)S(1)} %get-tuple-element.27), channel_id=1, source_target_pairs={{2,0},{4,2},{6,4},{3,1},{5,3},{7,5},{10,8},{12,10},{14,12},{11,9},... | collective-permute-start | bytes 98312 | tf_op jit(solution)/shard_map/ppermute | solution.py:22
  231.4 5.8 %collective-permute-start.47 = (f32[66,1,128]{2,1,0:T(1,128)S(1)}, f32[66,1,128]{2,1,0:T(1,128)S(1)}, u32[]{:S(2)}, u32[]{:S(2)}) collective-permute-start(f32[66,1,128]{2,1,0:T(1,128)S(1)} %get-tuple-element.13), channel_id=1, source_target_pairs={{1,0},{3,2},{5,4},{7,6},{9,8},{11,10},{13,12},{15,14},{17,16},{19,... | collective-permute-start | bytes 101384 | tf_op jit(solution)/shard_map/ppermute | solution.py:22
  240.7 3.5 %collective-permute-start.48 = (f32[1,64,128]{2,1,0:T(8,128)S(1)}, f32[1,64,128]{2,1,0:T(8,128)S(1)}, u32[]{:S(2)}, u32[]{:S(2)}) collective-permute-start(f32[1,64,128]{2,1,0:T(8,128)S(1)} %get-tuple-element.24), channel_id=1, source_target_pairs={{0,2},{2,4},{4,6},{1,3},{3,5},{5,7},{8,10},{10,12},{12,14},{9,11},... | collective-permute-start | bytes 98312 | tf_op jit(solution)/shard_map/ppermute | solution.py:19
  242.6 5.8 %collective-permute-start.49 = (f32[1,64,128]{2,1,0:T(8,128)S(1)}, f32[1,64,128]{2,1,0:T(8,128)S(1)}, u32[]{:S(2)}, u32[]{:S(2)}) collective-permute-start(f32[1,64,128]{2,1,0:T(8,128)S(1)} %get-tuple-element.25), channel_id=1, source_target_pairs={{2,0},{4,2},{6,4},{3,1},{5,3},{7,5},{10,8},{12,10},{14,12},{11,9},... | collective-permute-start | bytes 98312 | tf_op jit(solution)/shard_map/ppermute | solution.py:22
  250.1 5.8 %collective-permute-start.51 = (f32[66,1,128]{2,1,0:T(1,128)S(1)}, f32[66,1,128]{2,1,0:T(1,128)S(1)}, u32[]{:S(2)}, u32[]{:S(2)}) collective-permute-start(f32[66,1,128]{2,1,0:T(1,128)S(1)} %get-tuple-element.11), channel_id=1, source_target_pairs={{1,0},{3,2},{5,4},{7,6},{9,8},{11,10},{13,12},{15,14},{17,16},{19,... | collective-permute-start | bytes 101384 | tf_op jit(solution)/shard_map/ppermute | solution.py:22
  259.3 3.5 %collective-permute-start.52 = (f32[1,64,128]{2,1,0:T(8,128)S(1)}, f32[1,64,128]{2,1,0:T(8,128)S(1)}, u32[]{:S(2)}, u32[]{:S(2)}) collective-permute-start(f32[1,64,128]{2,1,0:T(8,128)S(1)} %get-tuple-element.22), channel_id=1, source_target_pairs={{0,2},{2,4},{4,6},{1,3},{3,5},{5,7},{8,10},{10,12},{12,14},{9,11},... | collective-permute-start | bytes 98312 | tf_op jit(solution)/shard_map/ppermute | solution.py:19
  261.2 5.8 %collective-permute-start.53 = (f32[1,64,128]{2,1,0:T(8,128)S(1)}, f32[1,64,128]{2,1,0:T(8,128)S(1)}, u32[]{:S(2)}, u32[]{:S(2)}) collective-permute-start(f32[1,64,128]{2,1,0:T(8,128)S(1)} %get-tuple-element.23), channel_id=1, source_target_pairs={{2,0},{4,2},{6,4},{3,1},{5,3},{7,5},{10,8},{12,10},{14,12},{11,9},... | collective-permute-start | bytes 98312 | tf_op jit(solution)/shard_map/ppermute | solution.py:22
  268.7 5.8 %collective-permute-start.55 = (f32[66,1,128]{2,1,0:T(1,128)S(1)}, f32[66,1,128]{2,1,0:T(1,128)S(1)}, u32[]{:S(2)}, u32[]{:S(2)}) collective-permute-start(f32[66,1,128]{2,1,0:T(1,128)S(1)} %get-tuple-element.9), channel_id=1, source_target_pairs={{1,0},{3,2},{5,4},{7,6},{9,8},{11,10},{13,12},{15,14},{17,16},{19,... | collective-permute-start | bytes 101384 | tf_op jit(solution)/shard_map/ppermute | solution.py:22
  (16 other events, 101.2 us)
where the time goes:
time: 280 us; the launch traced here: 279 us
  waiting for transfers between devices  111 us (40%)
  starting transfers between devices  101 us (36%)
  other arithmetic  60 us (21%)
  local copies, waits for them, and re-layouts  5.86 us (2%)
    ppermute x28, waiting for transfers between devices, with_halo(): lax.ppermute(lax.slice_in_dim(block, 0, width, axis=dim), axis, backward)  104 us
    ppermute x28, starting transfers between devices, with_halo(): lax.ppermute(lax.slice_in_dim(block, block.shape[dim] - width, None, axis...  64.9 us
    ppermute x28, starting transfers between devices, with_halo(): lax.ppermute(lax.slice_in_dim(block, 0, width, axis=dim), axis, backward)  36.4 us
    add x12, other arithmetic, sweep_once(): values + 0.8 * (load + neighbour_sum(padded) - (4.0 + mass_here) * values...  35.4 us
    sub x1, other arithmetic, per_device(): source_terms + neighbour_sum(with_halo(values, (('band', 0), ('lane', 1))...  9.31 us
    select_n x6, other arithmetic, per_device(): once = jnp.where(without_rim(inside), once, 0.0)  7.3 us
    ppermute x28, waiting for transfers between devices, with_halo(): lax.ppermute(lax.slice_in_dim(block, block.shape[dim] - width, None, axis...  6.77 us
  transfers between devices with their start and end apart: 56, of which 50 were waited for; matrix products, arithmetic and copies ran while one was open for 1% of the time, Pallas kernels for 0%

commit v1 on v0

v1 whole, which is shorter than its diff:
```python
import functools

import jax
import jax.numpy as jnp
from jax import lax
from jax.experimental import pallas as pl
from jax.experimental.pallas import tpu as pltpu
from jax.sharding import PartitionSpec as P

RATIO = 2
BEFORE = 3
AFTER = 3
INNER = 13
HALO = 8
ROWS = 2
SUB = 8
MESH = pl.DeviceIdType.MESH
DIRS = [(-1, 0), (1, 0), (0, -1), (0, 1), (-1, -1), (-1, 1), (1, -1), (1, 1)]

TRADES = [
    ("u_first", "fine", 2),
    ("w", "fine", 1),
    ("f", "fine", 1),
    ("cw", "coarse", 7),
    ("u_second", "fine", 2),
    ("cf", "coarse", 7),
    ("cu", "coarse", 6),
    ("u_third", "fine", 2),
]


class Grid:
    def __init__(self, rows, columns, row_halo, column_halo):
        self.rows, self.columns = rows, columns
        self.row_halo, self.column_halo = row_halo, column_halo
        self.pieces = (columns + 2 * column_halo) // SUB
        self.width = self.pieces * SUB
        self.stored = (rows + 2 * row_halo) * self.width

    def at(self, column):
        return (column % self.pieces) * SUB + column // self.pieces


def kernel(grids, src_hbm, init_hbm, abs_hbm, out_hbm, *scratch):
    fine, coarse = grids["fine"], grids["coarse"]
    raw = scratch[:3]
    u, v, w, f, iw, out, cw, cf, ca, cb, in_sem, out_sem, send_sem, recv_sem = scratch[3:17]
    lands = scratch[17:]
    band, lane = lax.axis_index("band"), lax.axis_index("lane")
    bands, lanes = lax.axis_size("band"), lax.axis_size("lane")

    def exists(q):
        dy, dx = q
        there = jnp.bool_(True)
        if dy:
            there = (band > 0) if dy < 0 else (band < bands - 1)
        if dx:
            beside = (lane > 0) if dx < 0 else (lane < lanes - 1)
            there = beside if not dy else there & beside
        return there

    def name_of(q):
        return {"band": band + q[0], "lane": lane + q[1]}

    loads = [
        pltpu.make_async_copy(
            ref, raw[i].at[:, pl.ds(fine.column_halo, fine.columns), :], in_sem.at[i]
        )
        for i, ref in enumerate((abs_hbm, src_hbm, init_hbm))
    ]
    for copy in loads:
        copy.start()

    trades = {}
    for t, (name, which, depth) in enumerate(TRADES):
        trades[name] = (t, grids[which], depth) + tuple(lands[4 * t : 4 * t + 4])

    barrier = pltpu.get_barrier_semaphore()
    for q in DIRS:
        @pl.when(exists(q))
        def _():
            pl.semaphore_signal(barrier, inc=1, device_id=name_of(q), device_id_type=MESH)

    def landing(trade, q):
        t, g, depth, strips, rows, columns, corners = trade
        dy, dx = q
        if not dx:
            return rows.at[(dy + 1) // 2]
        if not dy:
            return columns.at[(dx + 1) // 2]
        return corners.at[(dy + 1) // 2 * 2 + (dx + 1) // 2]

    def source(trade, arr, q):
        t, g, depth, strips, rows, columns, corners = trade
        dy, dx = q
        if not dx:
            first = g.row_halo if dy < 0 else g.row_halo + g.rows - depth
            return arr.at[pl.ds(first * g.width, depth * g.width), :]
        strip = strips.at[(dx + 1) // 2]
        if not dy:
            return strip
        return strip.at[:, pl.ds(0 if dy < 0 else g.rows - SUB, SUB), :]

    for trade in trades.values():
        for q in DIRS:
            @pl.when(jnp.logical_not(exists(q)))
            def _():
                ref = landing(trade, q)
                ref[...] = jnp.zeros(ref.shape, jnp.float32)

    on_band = (band > 0).astype(jnp.int32) + (band < bands - 1).astype(jnp.int32)
    on_lane = (lane > 0).astype(jnp.int32) + (lane < lanes - 1).astype(jnp.int32)
    pl.semaphore_wait(barrier, (on_band + 1) * (on_lane + 1) - 1)

    def copy_of(trade, arr, q, arriving):
        t = trade[0]
        back = (-q[0], -q[1])
        i, j = DIRS.index(q), DIRS.index(back)
        return pltpu.make_async_remote_copy(
            src_ref=source(trade, arr, q if not arriving else back),
            dst_ref=landing(trade, back if not arriving else q),
            send_sem=send_sem.at[t * 8 + i],
            recv_sem=recv_sem.at[t * 8 + (i if arriving else j)],
            device_id=name_of(q),
            device_id_type=MESH,
        )

    def send(name, arr):
        trade = trades[name]
        t, g, depth, strips, rows, columns, corners = trade
        for q in DIRS[:2]:
            @pl.when(exists(q))
            def _():
                copy_of(trade, arr, q, False).start()
        for side in range(2):
            first = g.column_halo if side == 0 else g.column_halo + g.columns - depth
            for j in range(depth):
                for i in range(g.rows // SUB):
                    at = (g.row_halo + SUB * i) * g.width + g.at(first + j)
                    strips[side, j, pl.ds(SUB * i, SUB), :] = arr[
                        pl.ds(at, SUB, stride=g.width), :
                    ]
        for q in DIRS[2:]:
            @pl.when(exists(q))
            def _():
                copy_of(trade, arr, q, False).start()

    def receive(name, arr):
        trade = trades[name]
        t, g, depth, strips, rows, columns, corners = trade
        for q in DIRS:
            @pl.when(exists(q))
            def _():
                copy_of(trade, arr, q, False).wait_send()
                copy_of(trade, arr, q, True).wait_recv()
        for side in range(2):
            first = g.row_halo - depth if side == 0 else g.row_halo + g.rows
            arr[pl.ds(first * g.width, depth * g.width), :] = rows[side]
        for side in range(2):
            first = g.column_halo - depth if side == 0 else g.column_halo + g.columns
            for j in range(depth):
                place = g.at(first + j)
                for i in range(g.rows // SUB):
                    at = (g.row_halo + SUB * i) * g.width + place
                    arr[pl.ds(at, SUB, stride=g.width), :] = columns[
                        side, j, pl.ds(SUB * i, SUB), :
                    ]
                for end in range(2):
                    row = g.row_halo - depth if end == 0 else g.row_halo + g.rows
                    skip = SUB - depth if end == 0 else 0
                    arr[pl.ds(row * g.width + place, depth, stride=g.width), :] = corners[
                        end * 2 + side, j, pl.ds(skip, depth), :
                    ]

    def piece(ref, g, row, k):
        return ref[pl.ds(pl.multiple_of(row * g.width + k * SUB, SUB), SUB), :]

    def put(ref, g, row, k, value):
        ref[pl.ds(pl.multiple_of(row * g.width + k * SUB, SUB), SUB), :] = value

    def around(ref, g, row):
        here = [piece(ref, g, row, k) for k in range(g.pieces)]
        before = [pltpu.roll(here[-1], 1, 0)] + here[:-1]
        after = here[1:] + [pltpu.roll(here[0], SUB - 1, 0)]
        sums = [
            (piece(ref, g, row - 1, k) + piece(ref, g, row + 1, k)) + (before[k] + after[k])
            for k in range(g.pieces)
        ]
        return here, sums

    def sweep(g, old, new, weight, load, wider):
        @pl.loop(g.row_halo - wider, g.row_halo + g.rows + wider, unroll=2)
        def _(row):
            here, sums = around(old, g, row)
            for k in range(g.pieces):
                value = (
                    0.2 * here[k] + piece(load, g, row, k) + piece(weight, g, row, k) * sums[k]
                )
                if new is out:
                    new[pl.ds((row - g.row_halo) * g.width + k, SUB, stride=g.pieces), :] = value
                else:
                    put(new, g, row, k, value)

    loads[0].wait()

    @pl.loop(0, coarse.rows)
    def _(row):
        total = [0.0] * coarse.pieces
        for half in range(RATIO):
            at = RATIO * row + half
            for k in range(fine.pieces):
                g4 = 4.0 + raw[0][at, pl.ds(k, SUB, stride=fine.pieces), :]
                put(w, fine, at + fine.row_halo, k, 0.8 / g4)
                put(iw, fine, at, k, 1.25 * g4)
                total[k // RATIO] = total[k // RATIO] + g4
        for k in range(coarse.pieces):
            mean = total[k] * (1.0 / RATIO) - (4.0 * RATIO - 4.0)
            put(cw, coarse, row + coarse.row_halo, k, 0.8 / mean)

    send("w", w)
    loads[2].wait()

    @pl.loop(0, fine.rows, unroll=2)
    def _(row):
        for k in range(fine.pieces):
            put(u, fine, row + fine.row_halo, k, raw[2][row, pl.ds(k, SUB, stride=fine.pieces), :])

    send("u_first", u)
    loads[1].wait()

    @pl.loop(0, fine.rows, unroll=2)
    def _(row):
        for k in range(fine.pieces):
            at = row + fine.row_halo
            put(f, fine, at, k, piece(w, fine, at, k) * raw[1][row, pl.ds(k, SUB, stride=fine.pieces), :])

    send("f", f)
    send("cw", cw)
    receive("w", w)
    receive("u_first", u)
    receive("f", f)
    sweep(fine, u, v, w, f, 1)
    sweep(fine, v, u, w, f, 0)
    send("u_second", u)
    receive("u_second", u)
    sweep(fine, u, v, w, f, 1)

    @pl.loop(0, coarse.rows)
    def _(row):
        total = [0.0] * coarse.pieces
        for half in range(RATIO):
            at = RATIO * row + half + fine.row_halo
            here, sums = around(v, fine, at)
            for k in range(fine.pieces):
                change = piece(f, fine, at, k) + piece(w, fine, at, k) * sums[k] - 0.8 * here[k]
                total[k // RATIO] = total[k // RATIO] + change * piece(
                    iw, fine, at - fine.row_halo, k
                )
        for k in range(coarse.pieces):
            at = row + coarse.row_halo
            put(cf, coarse, at, k, total[k] * (1.0 / RATIO) * piece(cw, coarse, at, k))

    send("cf", cf)
    receive("cw", cw)
    receive("cf", cf)
    old, new, spare = cf, ca, cb
    left = INNER - 1
    wider = 7
    while wider > 0:
        wider -= 1
        sweep(coarse, old, new, cw, cf, wider)
        old, new, spare = new, spare, new
        left -= 1
    send("cu", old)
    receive("cu", old)
    new = ca if old is cb else cb
    wider = 6
    while left > 0:
        wider -= 1
        sweep(coarse, old, new, cw, cf, wider)
        old, new = new, old
        left -= 1

    @pl.loop(-1, coarse.rows + 1)
    def _(row):
        for k in range(coarse.pieces):
            more = piece(old, coarse, row + coarse.row_halo, k)
            for half in range(RATIO):
                at = RATIO * row + half + fine.row_halo
                for part in range(RATIO):
                    put(v, fine, at, RATIO * k + part, piece(v, fine, at, RATIO * k + part) + more)

    sweep(fine, v, u, w, f, 0)
    send("u_third", u)
    receive("u_third", u)
    sweep(fine, u, v, w, f, 1)
    sweep(fine, v, out, w, f, 0)
    store = pltpu.make_async_copy(
        out.reshape(fine.rows, fine.width, 128).at[:, pl.ds(fine.column_halo, fine.columns), :],
        out_hbm,
        out_sem,
    )
    store.start()
    store.wait()


def per_device(source_terms, initial_values, absorption):
    rows, columns, cases = source_terms.shape
    fine = Grid(rows, columns, ROWS, RATIO * HALO)
    coarse = Grid(rows // RATIO, columns // RATIO, HALO, HALO)
    grids = {"fine": fine, "coarse": coarse}

    def held(*shape):
        return pltpu.VMEM(shape + (cases,), jnp.float32)

    shapes = [held(rows, fine.width) for _ in range(3)]
    shapes += [held(fine.stored) for _ in range(4)]
    shapes += [held(rows * fine.width), held(rows * fine.width)]
    shapes += [held(coarse.stored) for _ in range(4)]
    count = len(TRADES) * len(DIRS)
    shapes += [
        pltpu.SemaphoreType.DMA((3,)),
        pltpu.SemaphoreType.DMA,
        pltpu.SemaphoreType.DMA((count,)),
        pltpu.SemaphoreType.DMA((count,)),
    ]
    for name, which, depth in TRADES:
        g = grids[which]
        shapes += [
            held(2, depth, g.rows),
            held(2, depth * g.width),
            held(2, depth, g.rows),
            held(4, depth, SUB),
        ]
    return pl.pallas_call(
        functools.partial(kernel, grids),
        out_shape=jax.ShapeDtypeStruct(source_terms.shape, jnp.float32),
        in_specs=[pl.BlockSpec(memory_space=pl.ANY)] * 3,
        out_specs=pl.BlockSpec(memory_space=pl.ANY),
        scratch_shapes=shapes,
        compiler_params=pltpu.CompilerParams(
            collective_id=0, has_side_effects=True, vmem_limit_bytes=60 * 1024 * 1024
        ),
    )(source_terms, initial_values, absorption)


def solution(mesh):
    placed = P(("shift", "band"), "lane", None)
    return jax.shard_map(
        per_device,
        mesh=mesh,
        in_specs=(placed, placed, placed),
        out_specs=placed,
        check_vma=False,
    )
```

time: 280 us -> 50.4 us (0.18)
  waiting for transfers between devices: 111 us -> 0 us
  starting transfers between devices: 101 us -> 0 us
  other arithmetic: 60 us -> 0 us
  Pallas kernels: 0 us -> 47.1 us
    ppermute x56 -> x0, waiting for transfers between devices: 111 us -> none  [the longest x28 104 us: with_halo(): lax.ppermute(lax.slice_in_dim(block, 0, width, axis=dim), axis, backward)]
    ppermute x56 -> x0, starting transfers between devices: 101 us -> none  [the longest x28 64.9 us: with_halo(): lax.ppermute(lax.slice_in_dim(block, block.shape[dim] - width, None, axis...]
    pallas_call x0 -> x1, Pallas kernels: none -> 47.1 us  [per_device(): pl.pallas_call(functools.partial(kernel, grids), out_shape=jax.ShapeDtype...]
    add x13 -> x0, other arithmetic: 36 us -> none  [the longest x12 35.4 us: sweep_once(): values + 0.8 * (load + neighbour_sum(padded) - (4.0 + mass_here) * values...]
    sub x1 -> x0, other arithmetic: 9.31 us -> none  [per_device(): source_terms + neighbour_sum(with_halo(values, (('band', 0), ('lane', 1))...]
    select_n x6 -> x0, other arithmetic: 7.3 us -> none  [per_device(): once = jnp.where(without_rim(inside), once, 0.0)]
    reduce_sum x2 -> x0, other arithmetic: 4.89 us -> none  [block_means(): return jnp.mean(cut, axis=(1, 3))]
  transfers between devices with their start and end apart: 56 -> 0, of which waited for: 50 -> 0; matrix products, arithmetic and copies ran while one was open for 1% -> 0% of each run, Pallas kernels for 0% -> 0%
where the time goes in v1:
time: 50.4 us; the launch traced here: 50.2 us
  Pallas kernels  47.1 us (93%)
  local copies, waits for them, and re-layouts  3.16 us (6%)
    pallas_call x1, Pallas kernels, per_device(): pl.pallas_call(functools.partial(kernel, grids), out_shape=jax.ShapeDtype...  47.1 us
    unnamed x1, local copies, waits for them, and re-layouts  3.16 us

profile of v1, /device:TPU:0, one launch (start us, length us, event | category | flops | bytes accessed | tf_op | source)
XLA Modules:
  0.0 50.2 jit_solution(7414038083960128675)
XLA Ops:
  0.0 47.1 %shard_map.37 = f32[64,64,128]{2,1,0:T(8,128)} custom-call(f32[64,64,128]{2,1,0:T(8,128)} %src_hbm.1, f32[64,64,128]{2,1,0:T(8,128)} %init_hbm.1, f32[64,64,128]{2,1,0:T(8,128)} %abs_hbm.1), custom_call_target="tpu_custom_call" | custom-call | tf_op jit(solution)/shard_map/pallas_call | solution.py:335
  47.1 3.2 %copy.5 = f32[64,64,128]{2,1,0:T(8,128)} copy(f32[64,64,128]{2,1,0:T(8,128)} %shard_map.37) | data formatting | bytes 4194304

commit v2 on v1

--- a/solution.py
+++ b/solution.py
@@ -64,16 +64,18 @@
 
     loads = [
         pltpu.make_async_copy(
-            ref, raw[i].at[:, pl.ds(fine.column_halo, fine.columns), :], in_sem.at[i]
+            ref,
+            raw[i].reshape(fine.rows, fine.width, 128).at[:, pl.ds(fine.column_halo, fine.columns), :],
+            in_sem.at[i],
         )
         for i, ref in enumerate((abs_hbm, src_hbm, init_hbm))
     ]
-    for copy in loads:
-        copy.start()
+    for i in (2, 0, 1):
+        loads[i].start()
 
     trades = {}
     for t, (name, which, depth) in enumerate(TRADES):
-        trades[name] = (t, grids[which], depth) + tuple(lands[4 * t : 4 * t + 4])
+        trades[name] = (t, grids[which], depth) + tuple(lands[5 * t : 5 * t + 5])
 
     barrier = pltpu.get_barrier_semaphore()
     for q in DIRS:
@@ -82,20 +84,19 @@
             pl.semaphore_signal(barrier, inc=1, device_id=name_of(q), device_id_type=MESH)
 
     def landing(trade, q):
-        t, g, depth, strips, rows, columns, corners = trade
+        t, g, depth, sides, strips, rows, columns, corners = trade
         dy, dx = q
         if not dx:
-            return rows.at[(dy + 1) // 2]
+            return rows.at[(dy + 1) // 2, :, pl.ds(g.column_halo, g.columns), :]
         if not dy:
             return columns.at[(dx + 1) // 2]
         return corners.at[(dy + 1) // 2 * 2 + (dx + 1) // 2]
 
-    def source(trade, arr, q):
-        t, g, depth, strips, rows, columns, corners = trade
+    def source(trade, q):
+        t, g, depth, sides, strips, rows, columns, corners = trade
         dy, dx = q
         if not dx:
-            first = g.row_halo if dy < 0 else g.row_halo + g.rows - depth
-            return arr.at[pl.ds(first * g.width, depth * g.width), :]
+            return sides.at[(dy + 1) // 2, :, pl.ds(g.column_halo, g.columns), :]
         strip = strips.at[(dx + 1) // 2]
         if not dy:
             return strip
@@ -112,12 +113,12 @@
     on_lane = (lane > 0).astype(jnp.int32) + (lane < lanes - 1).astype(jnp.int32)
     pl.semaphore_wait(barrier, (on_band + 1) * (on_lane + 1) - 1)
 
-    def copy_of(trade, arr, q, arriving):
+    def copy_of(trade, q, arriving):
         t = trade[0]
         back = (-q[0], -q[1])
         i, j = DIRS.index(q), DIRS.index(back)
         return pltpu.make_async_remote_copy(
-            src_ref=source(trade, arr, q if not arriving else back),
+            src_ref=source(trade, q if not arriving else back),
             dst_ref=landing(trade, back if not arriving else q),
             send_sem=send_sem.at[t * 8 + i],
             recv_sem=recv_sem.at[t * 8 + (i if arriving else j)],
@@ -125,13 +126,21 @@
             device_id_type=MESH,
         )
 
+    def start(trade, directions):
+        for q in directions:
+            @pl.when(exists(q))
+            def _():
+                copy_of(trade, q, False).start()
+
     def send(name, arr):
         trade = trades[name]
-        t, g, depth, strips, rows, columns, corners = trade
-        for q in DIRS[:2]:
-            @pl.when(exists(q))
-            def _():
-                copy_of(trade, arr, q, False).start()
+        t, g, depth, sides, strips, rows, columns, corners = trade
+        for side in range(2):
+            first = g.row_halo if side == 0 else g.row_halo + g.rows - depth
+            for i in range(depth):
+                for k in range(g.pieces):
+                    sides[side, i, pl.ds(k, SUB, stride=g.pieces), :] = piece(arr, g, first + i, k)
+        start(trade, DIRS[:2])
         for side in range(2):
             first = g.column_halo if side == 0 else g.column_halo + g.columns - depth
             for j in range(depth):
@@ -140,22 +149,42 @@
                     strips[side, j, pl.ds(SUB * i, SUB), :] = arr[
                         pl.ds(at, SUB, stride=g.width), :
                     ]
-        for q in DIRS[2:]:
-            @pl.when(exists(q))
-            def _():
-                copy_of(trade, arr, q, False).start()
+        start(trade, DIRS[2:])
+
+    def send_raw(name, value):
+        trade = trades[name]
+        t, g, depth, sides, strips, rows, columns, corners = trade
+        for side in range(2):
+            first = 0 if side == 0 else g.rows - depth
+            for i in range(depth):
+                for c in range(g.columns // SUB):
+                    at = g.column_halo + SUB * c
+                    sides[side, i, pl.ds(at, SUB), :] = value(
+                        lambda ref: ref[pl.ds((first + i) * g.width + at, SUB), :]
+                    )
+        start(trade, DIRS[:2])
+        for side in range(2):
+            first = g.column_halo if side == 0 else g.column_halo + g.columns - depth
+            for j in range(depth):
+                for i in range(g.rows // SUB):
+                    strips[side, j, pl.ds(SUB * i, SUB), :] = value(
+                        lambda ref: ref[pl.ds(SUB * i * g.width + first + j, SUB, stride=g.width), :]
+                    )
+        start(trade, DIRS[2:])
 
     def receive(name, arr):
         trade = trades[name]
-        t, g, depth, strips, rows, columns, corners = trade
+        t, g, depth, sides, strips, rows, columns, corners = trade
         for q in DIRS:
             @pl.when(exists(q))
             def _():
-                copy_of(trade, arr, q, False).wait_send()
-                copy_of(trade, arr, q, True).wait_recv()
+                copy_of(trade, q, False).wait_send()
+                copy_of(trade, q, True).wait_recv()
         for side in range(2):
             first = g.row_halo - depth if side == 0 else g.row_halo + g.rows
-            arr[pl.ds(first * g.width, depth * g.width), :] = rows[side]
+            for i in range(depth):
+                for k in range(g.pieces):
+                    put(arr, g, first + i, k, rows[side, i, pl.ds(k, SUB, stride=g.pieces), :])
         for side in range(2):
             first = g.column_halo - depth if side == 0 else g.column_halo + g.columns
             for j in range(depth):
@@ -201,7 +230,12 @@
                 else:
                     put(new, g, row, k, value)
 
+    loads[2].wait()
+    send_raw("u_first", lambda read: read(raw[2]))
     loads[0].wait()
+    send_raw("w", lambda read: 0.8 / (4.0 + read(raw[0])))
+    loads[1].wait()
+    send_raw("f", lambda read: 0.8 / (4.0 + read(raw[0])) * read(raw[1]))
 
     @pl.loop(0, coarse.rows)
     def _(row):
@@ -209,7 +243,7 @@
         for half in range(RATIO):
             at = RATIO * row + half
             for k in range(fine.pieces):
-                g4 = 4.0 + raw[0][at, pl.ds(k, SUB, stride=fine.pieces), :]
+                g4 = 4.0 + raw[0][pl.ds(at * fine.width + k, SUB, stride=fine.pieces), :]
                 put(w, fine, at + fine.row_halo, k, 0.8 / g4)
                 put(iw, fine, at, k, 1.25 * g4)
                 total[k // RATIO] = total[k // RATIO] + g4
@@ -217,25 +251,20 @@
             mean = total[k] * (1.0 / RATIO) - (4.0 * RATIO - 4.0)
             put(cw, coarse, row + coarse.row_halo, k, 0.8 / mean)
 
-    send("w", w)
-    loads[2].wait()
+    send("cw", cw)
 
     @pl.loop(0, fine.rows, unroll=2)
     def _(row):
         for k in range(fine.pieces):
-            put(u, fine, row + fine.row_halo, k, raw[2][row, pl.ds(k, SUB, stride=fine.pieces), :])
-
-    send("u_first", u)
-    loads[1].wait()
+            put(u, fine, row + fine.row_halo, k, raw[2][pl.ds(row * fine.width + k, SUB, stride=fine.pieces), :])
+
 
     @pl.loop(0, fine.rows, unroll=2)
     def _(row):
         for k in range(fine.pieces):
             at = row + fine.row_halo
-            put(f, fine, at, k, piece(w, fine, at, k) * raw[1][row, pl.ds(k, SUB, stride=fine.pieces), :])
-
-    send("f", f)
-    send("cw", cw)
+            put(f, fine, at, k, piece(w, fine, at, k) * raw[1][pl.ds(row * fine.width + k, SUB, stride=fine.pieces), :])
+
     receive("w", w)
     receive("u_first", u)
     receive("f", f)
@@ -313,7 +342,7 @@
     def held(*shape):
         return pltpu.VMEM(shape + (cases,), jnp.float32)
 
-    shapes = [held(rows, fine.width) for _ in range(3)]
+    shapes = [held(rows * fine.width) for _ in range(3)]
     shapes += [held(fine.stored) for _ in range(4)]
     shapes += [held(rows * fine.width), held(rows * fine.width)]
     shapes += [held(coarse.stored) for _ in range(4)]
@@ -327,8 +356,9 @@
     for name, which, depth in TRADES:
         g = grids[which]
         shapes += [
+            held(2, depth, g.width),
             held(2, depth, g.rows),
-            held(2, depth * g.width),
+            held(2, depth, g.width),
             held(2, depth, g.rows),
             held(4, depth, SUB),
         ]

time: 50.4 us -> 46.2 us (0.917)
  Pallas kernels: 47.1 us -> 42.9 us
    pallas_call x1, Pallas kernels: 47.1 us -> 42.9 us  [per_device(): pl.pallas_call(functools.partial(kernel, grids), out_shape=jax.ShapeDtype...]
where the time goes in v2:
time: 46.2 us; the launch traced here: 46 us
  Pallas kernels  42.9 us (93%)
  local copies, waits for them, and re-layouts  3.16 us (7%)
    pallas_call x1, Pallas kernels, per_device(): pl.pallas_call(functools.partial(kernel, grids), out_shape=jax.ShapeDtype...  42.9 us
    unnamed x1, local copies, waits for them, and re-layouts  3.16 us

profile of v2, /device:TPU:0, one launch (start us, length us, event | category | flops | bytes accessed | tf_op | source)
XLA Modules:
  0.0 46.0 jit_solution(4095158649097158092)
XLA Ops:
  0.0 42.9 %shard_map.37 = f32[64,64,128]{2,1,0:T(8,128)} custom-call(f32[64,64,128]{2,1,0:T(8,128)} %src_hbm.1, f32[64,64,128]{2,1,0:T(8,128)} %init_hbm.1, f32[64,64,128]{2,1,0:T(8,128)} %abs_hbm.1), custom_call_target="tpu_custom_call" | custom-call | tf_op jit(solution)/shard_map/pallas_call | solution.py:365
  42.9 3.2 %copy.5 = f32[64,64,128]{2,1,0:T(8,128)} copy(f32[64,64,128]{2,1,0:T(8,128)} %shard_map.37) | data formatting | bytes 4194304

commit v3 on v2

--- a/solution.py
+++ b/solution.py
@@ -15,6 +15,8 @@
 ROWS = 2
 SUB = 8
 MESH = pl.DeviceIdType.MESH
+CHUNKS = 4
+BLOCK = 4
 DIRS = [(-1, 0), (1, 0), (0, -1), (0, 1), (-1, -1), (-1, 1), (1, -1), (1, 1)]
 
 TRADES = [
@@ -136,12 +138,6 @@
         trade = trades[name]
         t, g, depth, sides, strips, rows, columns, corners = trade
         for side in range(2):
-            first = g.row_halo if side == 0 else g.row_halo + g.rows - depth
-            for i in range(depth):
-                for k in range(g.pieces):
-                    sides[side, i, pl.ds(k, SUB, stride=g.pieces), :] = piece(arr, g, first + i, k)
-        start(trade, DIRS[:2])
-        for side in range(2):
             first = g.column_halo if side == 0 else g.column_halo + g.columns - depth
             for j in range(depth):
                 for i in range(g.rows // SUB):
@@ -149,11 +145,27 @@
                     strips[side, j, pl.ds(SUB * i, SUB), :] = arr[
                         pl.ds(at, SUB, stride=g.width), :
                     ]
-        start(trade, DIRS[2:])
+        start(trade, DIRS[4:])
+        start(trade, DIRS[2:4])
+        for side in range(2):
+            first = g.row_halo if side == 0 else g.row_halo + g.rows - depth
+            for i in range(depth):
+                for k in range(g.pieces):
+                    sides[side, i, pl.ds(k, SUB, stride=g.pieces), :] = piece(arr, g, first + i, k)
+        start(trade, DIRS[:2])
 
     def send_raw(name, value):
         trade = trades[name]
         t, g, depth, sides, strips, rows, columns, corners = trade
+        for side in range(2):
+            first = g.column_halo if side == 0 else g.column_halo + g.columns - depth
+            for j in range(depth):
+                for i in range(g.rows // SUB):
+                    strips[side, j, pl.ds(SUB * i, SUB), :] = value(
+                        lambda ref: ref[pl.ds(SUB * i * g.width + first + j, SUB, stride=g.width), :]
+                    )
+        start(trade, DIRS[4:])
+        start(trade, DIRS[2:4])
         for side in range(2):
             first = 0 if side == 0 else g.rows - depth
             for i in range(depth):
@@ -163,14 +175,6 @@
                         lambda ref: ref[pl.ds((first + i) * g.width + at, SUB), :]
                     )
         start(trade, DIRS[:2])
-        for side in range(2):
-            first = g.column_halo if side == 0 else g.column_halo + g.columns - depth
-            for j in range(depth):
-                for i in range(g.rows // SUB):
-                    strips[side, j, pl.ds(SUB * i, SUB), :] = value(
-                        lambda ref: ref[pl.ds(SUB * i * g.width + first + j, SUB, stride=g.width), :]
-                    )
-        start(trade, DIRS[2:])
 
     def receive(name, arr):
         trade = trades[name]
@@ -217,18 +221,60 @@
         ]
         return here, sums
 
-    def sweep(g, old, new, weight, load, wider):
-        @pl.loop(g.row_halo - wider, g.row_halo + g.rows + wider, unroll=2)
-        def _(row):
-            here, sums = around(old, g, row)
-            for k in range(g.pieces):
+    def block(g, old, new, weight, load, row, count, ks):
+        seen = {}
+
+        def get(i, k):
+            if (i, k) not in seen:
+                seen[i, k] = piece(old, g, row + i, k)
+            return seen[i, k]
+
+        for k in ks:
+            for i in range(count):
+                left = get(i, k - 1) if k else pltpu.roll(get(i, g.pieces - 1), 1, 0)
+                right = get(i, k + 1) if k < g.pieces - 1 else pltpu.roll(get(i, 0), SUB - 1, 0)
+                total = (get(i - 1, k) + get(i + 1, k)) + (left + right)
                 value = (
-                    0.2 * here[k] + piece(load, g, row, k) + piece(weight, g, row, k) * sums[k]
+                    0.2 * get(i, k)
+                    + piece(load, g, row + i, k)
+                    + piece(weight, g, row + i, k) * total
                 )
                 if new is out:
-                    new[pl.ds((row - g.row_halo) * g.width + k, SUB, stride=g.pieces), :] = value
+                    at = (row + i - g.row_halo) * g.width + k
+                    new[pl.ds(at, SUB, stride=g.pieces), :] = value
                 else:
-                    put(new, g, row, k, value)
+                    put(new, g, row + i, k, value)
+
+    def part(g, old, new, weight, load, first, last, ks):
+        whole = (last - first) // BLOCK
+
+        @pl.loop(0, whole)
+        def _(b):
+            block(g, old, new, weight, load, first + BLOCK * b, BLOCK, ks)
+
+        if last - first > whole * BLOCK:
+            at = first + whole * BLOCK
+            block(g, old, new, weight, load, at, last - at, ks)
+
+    def sweep(g, old, new, weight, load, wider):
+        part(g, old, new, weight, load, g.row_halo - wider, g.row_halo + g.rows + wider, range(g.pieces))
+
+    def near(g, outside, inside):
+        low = range(g.column_halo - outside, g.column_halo + inside)
+        high = range(g.column_halo + g.columns - inside, g.column_halo + g.columns + outside)
+        return sorted({c % g.pieces for c in (*low, *high)})
+
+    def edges(g, old, new, weight, load, outside, inside):
+        top, end = g.row_halo, g.row_halo + g.rows
+        every = range(g.pieces)
+        block(g, old, new, weight, load, top - outside, outside + inside, every)
+        block(g, old, new, weight, load, end - inside, outside + inside, every)
+        part(g, old, new, weight, load, top + inside, end - inside, near(g, outside, inside))
+
+    def inner(g, old, new, weight, load, inside):
+        ks = sorted(set(range(g.pieces)) - set(near(g, 0, inside)))
+        first, last = g.row_halo + inside, g.row_halo + g.rows - inside
+        part(g, old, new, weight, load, first, last, ks)
 
     loads[2].wait()
     send_raw("u_first", lambda read: read(raw[2]))
@@ -265,14 +311,17 @@
             at = row + fine.row_halo
             put(f, fine, at, k, piece(w, fine, at, k) * raw[1][pl.ds(row * fine.width + k, SUB, stride=fine.pieces), :])
 
+    sweep(fine, u, v, w, f, 0)
     receive("w", w)
     receive("u_first", u)
     receive("f", f)
-    sweep(fine, u, v, w, f, 1)
-    sweep(fine, v, u, w, f, 0)
+    edges(fine, u, v, w, f, 1, 1)
+    edges(fine, v, u, w, f, 0, 2)
     send("u_second", u)
+    inner(fine, v, u, w, f, 2)
+    sweep(fine, u, v, w, f, 0)
     receive("u_second", u)
-    sweep(fine, u, v, w, f, 1)
+    edges(fine, u, v, w, f, 1, 1)
 
     @pl.loop(0, coarse.rows)
     def _(row):
@@ -319,18 +368,29 @@
                 for part in range(RATIO):
                     put(v, fine, at, RATIO * k + part, piece(v, fine, at, RATIO * k + part) + more)
 
-    sweep(fine, v, u, w, f, 0)
+    edges(fine, v, u, w, f, 0, 2)
     send("u_third", u)
+    inner(fine, v, u, w, f, 2)
+    sweep(fine, u, v, w, f, 0)
     receive("u_third", u)
-    sweep(fine, u, v, w, f, 1)
-    sweep(fine, v, out, w, f, 0)
-    store = pltpu.make_async_copy(
-        out.reshape(fine.rows, fine.width, 128).at[:, pl.ds(fine.column_halo, fine.columns), :],
-        out_hbm,
-        out_sem,
-    )
-    store.start()
-    store.wait()
+    edges(fine, u, v, w, f, 1, 1)
+    stores = []
+    chunk = fine.rows // CHUNKS
+    for c in range(CHUNKS):
+        first = fine.row_halo + c * chunk
+        part(fine, v, out, w, f, first, first + chunk, range(fine.pieces))
+        stores.append(
+            pltpu.make_async_copy(
+                out.reshape(fine.rows, fine.width, 128).at[
+                    pl.ds(c * chunk, chunk), pl.ds(fine.column_halo, fine.columns), :
+                ],
+                out_hbm.at[pl.ds(c * chunk, chunk)],
+                out_sem.at[c],
+            )
+        )
+        stores[-1].start()
+    for store in stores:
+        store.wait()
 
 
 def per_device(source_terms, initial_values, absorption):
@@ -349,7 +409,7 @@
     count = len(TRADES) * len(DIRS)
     shapes += [
         pltpu.SemaphoreType.DMA((3,)),
-        pltpu.SemaphoreType.DMA,
+        pltpu.SemaphoreType.DMA((CHUNKS,)),
         pltpu.SemaphoreType.DMA((count,)),
         pltpu.SemaphoreType.DMA((count,)),
     ]

time: 46.2 us -> 41 us (0.89)
  Pallas kernels: 42.9 us -> 37.7 us
    pallas_call x1, Pallas kernels: 42.9 us -> 37.7 us  [per_device(): pl.pallas_call(functools.partial(kernel, grids), out_shape=jax.ShapeDtype...]
where the time goes in v3:
time: 41 us; the launch traced here: 40.8 us
  Pallas kernels  37.7 us (92%)
  local copies, waits for them, and re-layouts  3.16 us (8%)
    pallas_call x1, Pallas kernels, per_device(): pl.pallas_call(functools.partial(kernel, grids), out_shape=jax.ShapeDtype...  37.7 us
    unnamed x1, local copies, waits for them, and re-layouts  3.16 us

profile of v3, /device:TPU:0, one launch (start us, length us, event | category | flops | bytes accessed | tf_op | source)
XLA Modules:
  0.0 40.8 jit_solution(13252830357071643999)
XLA Ops:
  0.0 37.7 %shard_map.37 = f32[64,64,128]{2,1,0:T(8,128)} custom-call(f32[64,64,128]{2,1,0:T(8,128)} %src_hbm.1, f32[64,64,128]{2,1,0:T(8,128)} %init_hbm.1, f32[64,64,128]{2,1,0:T(8,128)} %abs_hbm.1), custom_call_target="tpu_custom_call" | custom-call | tf_op jit(solution)/shard_map/pallas_call | solution.py:425
  37.7 3.2 %copy.5 = f32[64,64,128]{2,1,0:T(8,128)} copy(f32[64,64,128]{2,1,0:T(8,128)} %shard_map.37) | data formatting | bytes 4194304

commit v4 on v3

--- a/solution.py
+++ b/solution.py
@@ -23,7 +23,7 @@
     ("u_first", "fine", 2),
     ("w", "fine", 1),
     ("f", "fine", 1),
-    ("cw", "coarse", 7),
+    ("cw", "coarse", 6),
     ("u_second", "fine", 2),
     ("cf", "coarse", 7),
     ("cu", "coarse", 6),
@@ -374,23 +374,15 @@
     sweep(fine, u, v, w, f, 0)
     receive("u_third", u)
     edges(fine, u, v, w, f, 1, 1)
-    stores = []
     chunk = fine.rows // CHUNKS
     for c in range(CHUNKS):
         first = fine.row_halo + c * chunk
         part(fine, v, out, w, f, first, first + chunk, range(fine.pieces))
-        stores.append(
-            pltpu.make_async_copy(
-                out.reshape(fine.rows, fine.width, 128).at[
-                    pl.ds(c * chunk, chunk), pl.ds(fine.column_halo, fine.columns), :
-                ],
-                out_hbm.at[pl.ds(c * chunk, chunk)],
-                out_sem.at[c],
-            )
-        )
-        stores[-1].start()
-    for store in stores:
-        store.wait()
+
+        @pl.loop(c * chunk, (c + 1) * chunk, unroll=4)
+        def _(row):
+            at = pl.multiple_of(row * fine.width + fine.column_halo, SUB)
+            out_hbm[row] = out[pl.ds(at, fine.columns), :]
 
 
 def per_device(source_terms, initial_values, absorption):
@@ -425,13 +417,13 @@
     return pl.pallas_call(
         functools.partial(kernel, grids),
         out_shape=jax.ShapeDtypeStruct(source_terms.shape, jnp.float32),
-        in_specs=[pl.BlockSpec(memory_space=pl.ANY)] * 3,
-        out_specs=pl.BlockSpec(memory_space=pl.ANY),
+        in_specs=[pl.BlockSpec(memory_space=pltpu.HBM)] * 3,
+        out_specs=pl.BlockSpec(memory_space=pltpu.VMEM),
         scratch_shapes=shapes,
         compiler_params=pltpu.CompilerParams(
-            collective_id=0, has_side_effects=True, vmem_limit_bytes=60 * 1024 * 1024
+            collective_id=0, has_side_effects=True, vmem_limit_bytes=44 * 1024 * 1024
         ),
-    )(source_terms, initial_values, absorption)
+    )(*[pltpu.with_memory_space_constraint(x, pltpu.HBM) for x in (source_terms, initial_values, absorption)])
 
 
 def solution(mesh):

time: 41 us -> 38.2 us (0.932)
  local copies, waits for them, and re-layouts: 3.16 us -> 1.32 us
  Pallas kernels: 37.7 us -> 36.8 us
    unnamed x1, local copies, waits for them, and re-layouts: 3.16 us -> 1.32 us
    pallas_call x1, Pallas kernels: 37.7 us -> 36.8 us  [per_device(): pl.pallas_call(functools.partial(kernel, grids), out_shape=jax.ShapeDtype...]
where the time goes in v4:
time: 38.2 us; the launch traced here: 38.1 us
  Pallas kernels  36.8 us (96%)
  local copies, waits for them, and re-layouts  1.32 us (3%)
    pallas_call x1, Pallas kernels, per_device(): pl.pallas_call(functools.partial(kernel, grids), out_shape=jax.ShapeDtype...  36.8 us
    unnamed x1, local copies, waits for them, and re-layouts  1.32 us

profile of v4, /device:TPU:0, one launch (start us, length us, event | category | flops | bytes accessed | tf_op | source)
XLA Modules:
  0.0 38.1 jit_solution(16884881196653533183)
XLA Ops:
  0.0 36.8 %shard_map.37 = f32[64,64,128]{2,1,0:T(8,128)S(1)} custom-call(f32[64,64,128]{2,1,0:T(8,128)} %src_hbm.1, f32[64,64,128]{2,1,0:T(8,128)} %init_hbm.1, f32[64,64,128]{2,1,0:T(8,128)} %abs_hbm.1), custom_call_target="tpu_custom_call" | custom-call | tf_op jit(solution)/shard_map/pallas_call | solution.py:417
  36.8 1.3 %copy.5 = f32[64,64,128]{2,1,0:T(8,128)} copy(f32[64,64,128]{2,1,0:T(8,128)S(1)} %shard_map.37) | data formatting | bytes 4194304

commit v5 on v4

--- a/solution.py
+++ b/solution.py
@@ -16,7 +16,7 @@
 SUB = 8
 MESH = pl.DeviceIdType.MESH
 CHUNKS = 4
-BLOCK = 4
+BLOCK = 8
 DIRS = [(-1, 0), (1, 0), (0, -1), (0, 1), (-1, -1), (-1, 1), (1, -1), (1, 1)]
 
 TRADES = [
@@ -297,7 +297,6 @@
             mean = total[k] * (1.0 / RATIO) - (4.0 * RATIO - 4.0)
             put(cw, coarse, row + coarse.row_halo, k, 0.8 / mean)
 
-    send("cw", cw)
 
     @pl.loop(0, fine.rows, unroll=2)
     def _(row):
@@ -318,6 +317,7 @@
     edges(fine, u, v, w, f, 1, 1)
     edges(fine, v, u, w, f, 0, 2)
     send("u_second", u)
+    send("cw", cw)
     inner(fine, v, u, w, f, 2)
     sweep(fine, u, v, w, f, 0)
     receive("u_second", u)

time: 38.2 us -> 37.4 us (0.979)
  Pallas kernels: 36.8 us -> 35.9 us
    pallas_call x1, Pallas kernels: 36.8 us -> 35.9 us  [per_device(): pl.pallas_call(functools.partial(kernel, grids), out_shape=jax.ShapeDtype...]
where the time goes in v5:
time: 37.4 us; the launch traced here: 37.2 us
  Pallas kernels  35.9 us (96%)
  local copies, waits for them, and re-layouts  1.32 us (4%)
    pallas_call x1, Pallas kernels, per_device(): pl.pallas_call(functools.partial(kernel, grids), out_shape=jax.ShapeDtype...  35.9 us
    unnamed x1, local copies, waits for them, and re-layouts  1.32 us

profile of v5, /device:TPU:0, one launch (start us, length us, event | category | flops | bytes accessed | tf_op | source)
XLA Modules:
  0.0 37.2 jit_solution(4222928457284232960)
XLA Ops:
  0.0 35.9 %shard_map.37 = f32[64,64,128]{2,1,0:T(8,128)S(1)} custom-call(f32[64,64,128]{2,1,0:T(8,128)} %src_hbm.1, f32[64,64,128]{2,1,0:T(8,128)} %init_hbm.1, f32[64,64,128]{2,1,0:T(8,128)} %abs_hbm.1), custom_call_target="tpu_custom_call" | custom-call | tf_op jit(solution)/shard_map/pallas_call | solution.py:417
  35.9 1.3 %copy.5 = f32[64,64,128]{2,1,0:T(8,128)} copy(f32[64,64,128]{2,1,0:T(8,128)S(1)} %shard_map.37) | data formatting | bytes 4194304
